TPU v7x, 32 devices: a whole 2x2x4 slice. The times are simulated.
32 devices in a mesh: mp: 4 (over z), space: 8 (over y, x, core).
Axes of the slice: x: 2, y: 2, z: 4, core: 2. Of those that a mesh axis runs over, the one named last changes fastest.
Arguments:
- positions: float32 [3, 512], P(None, 'space'), may hold values from 0 to 1
- send_lists: int32 [8, 6, 128], P('space'), may hold values from -1 to 575, as said below
- neighbours: int32 [96, 512], P(None, 'space'), may hold values from -1 to 831, as said below
- emb_scale: float32 [4, 25], P('mp'), may hold values from -4 to 4
- emb_shift: float32 [4, 25], P('mp'), may hold values from -4 to 4
- emb_middle: bfloat16 [4, 50, 25], P('mp'), may hold values from -1.25 to 1.25
- emb_mid_bias: float32 [4, 50], P('mp'), may hold values from -3 to 3
- emb_outer: bfloat16 [4, 100, 50], P('mp'), may hold values from -0.875 to 0.875
- emb_out_bias: float32 [4, 100], P('mp'), may hold values from -3 to 3
- fit_first: bfloat16 [4, 240, 1600], P('mp'), may hold values from -0.078125 to 0.078125
- fit_first_bias: float32 [4, 240], P('mp'), may hold values from -3 to 3
- fit_second: bfloat16 [4, 240, 240], P('mp'), may hold values from -0.375 to 0.375
- fit_second_bias: float32 [4, 240], P('mp'), may hold values from -3 to 3
- fit_third: bfloat16 [4, 240, 240], P('mp'), may hold values from -0.375 to 0.375
- fit_third_bias: float32 [4, 240], P('mp'), may hold values from -3 to 3
- fit_readout: bfloat16 [4, 240], P('mp'), may hold values from -0.375 to 0.375
Outputs:
- mean_force: float32 [3, 8, 4, 16], P(None, 'space', 'mp')
- force_spread: float32 [8, 4, 16], P('space', 'mp')
- virial_spread: float32 [8, 4, 16], P('space', 'mp')
Inputs may be any that keep to these rules, and one draw needn't show every extreme that they name: `send_lists`: direction b runs +x, -x, +y, -y, +z, -z. A list of section b // 2 names owned atoms (below 64) or live ghost slots of earlier sections of the sender's extended array; live entries come first and -1 fills the rest; each list holds 42 to 128 live entries, entries may repeat, and in every draw some domain's list in each direction is full. `neighbours`: each entry names another owned atom of the same domain or a live ghost slot of that domain's extended array; -1 marks an empty slot.
All inputs are finite; a program needn't handle non-finite values.
Results may differ from a plain program's by a relative error of at most 0.012.
Values sent between devices are 32-bit elements; how exact they have to be, the bound alone decides.
A program may use at most 64 MiB of HBM per device.

v0:
```python
import functools

import jax
import jax.numpy as jnp
from jax import lax
from jax.experimental import pallas as pl
from jax.experimental.pallas import tpu as pltpu
from jax.sharding import PartitionSpec as P

AXIS = 16
SOFTEN = 0.04
LANES = 128
MESH = pl.DeviceIdType.MESH
F32 = jnp.float32
BF16 = jnp.bfloat16
VM = pl.BlockSpec(memory_space=pltpu.VMEM)


def dims(space_count):
    grid_y = min(4, max(2, space_count // 16))
    strides = (grid_y * grid_y, grid_y, 1)
    span = (-1, 0, 1)
    found = sorted(
        {
            (a * strides[0] + b * strides[1] + c * strides[2]) % space_count
            for a in span
            for b in span
            for c in span
        }
    )
    return strides, found


def nn(a, b):
    return jnp.dot(a, b, preferred_element_type=F32)


def nt(a, b):
    return lax.dot_general(a, b, (((1,), (1,)), ((), ())), preferred_element_type=F32)


def tn(a, b):
    return lax.dot_general(a, b, (((0,), (0,)), ((), ())), preferred_element_type=F32)


def iota(shape, dim):
    return lax.broadcasted_iota(jnp.int32, shape, dim)


def hot(mask):
    return jnp.where(mask, 1.0, 0.0).astype(BF16)


def share_kernel(count, found, pos_ref, list_ref, pos_out, list_out, send_a, recv_a, send_b, recv_b):
    me = lax.axis_index("space")
    barrier = pltpu.get_barrier_semaphore()
    for off in found[1:]:
        pl.semaphore_signal(
            barrier, inc=1, device_id={"space": lax.rem(me + off, count)}, device_id_type=MESH
        )
    pl.semaphore_wait(barrier, len(found) - 1)
    copies = []
    for slot, off in enumerate(found):
        if off == 0:
            continue
        peer = lax.rem(me + count - off, count)
        for src, dst, send, recv in (
            (pos_ref, pos_out, send_a, recv_a),
            (list_ref, list_out, send_b, recv_b),
        ):
            copy = pltpu.make_async_remote_copy(
                src_ref=src,
                dst_ref=dst.at[slot],
                send_sem=send.at[slot],
                recv_sem=recv.at[slot],
                device_id={"space": peer},
                device_id_type=MESH,
            )
            copy.start()
            copies.append(copy)
    pos_out[0] = pos_ref[...]
    list_out[0] = list_ref[...]
    for copy in copies:
        copy.wait()


def share(positions, lists, count, found):
    slots = len(found)
    return pl.pallas_call(
        functools.partial(share_kernel, count, found),
        out_shape=(
            jax.ShapeDtypeStruct((slots,) + positions.shape, F32),
            jax.ShapeDtypeStruct((slots,) + lists.shape, jnp.int32),
        ),
        in_specs=[VM, VM],
        out_specs=(VM, VM),
        scratch_shapes=[pltpu.SemaphoreType.DMA((slots,))] * 4,
        compiler_params=pltpu.CompilerParams(collective_id=0, has_side_effects=True),
        name="share",
    )(positions, lists)


def reduce_kernel(count, models, found, part_ref, mean_ref, force_ref, virial_ref,
                  held, total, others, send_a, recv_a, send_b, recv_b):
    me = lax.axis_index("space")
    model = lax.axis_index("mp")
    barrier = pltpu.get_barrier_semaphore()
    for off in found[1:]:
        pl.semaphore_signal(
            barrier, inc=1, device_id={"space": lax.rem(me + off, count)}, device_id_type=MESH
        )
    for step in range(1, models):
        pl.semaphore_signal(
            barrier, inc=1, device_id={"mp": lax.rem(model + step, models)}, device_id_type=MESH
        )
    pl.semaphore_wait(barrier, len(found) - 1 + models - 1)
    copies = []
    for slot, off in enumerate(found):
        if off == 0:
            continue
        copy = pltpu.make_async_remote_copy(
            src_ref=part_ref.at[slot],
            dst_ref=held.at[slot],
            send_sem=send_a.at[slot],
            recv_sem=recv_a.at[slot],
            device_id={"space": lax.rem(me + off, count)},
            device_id_type=MESH,
        )
        copy.start()
        copies.append(copy)
    for copy in copies:
        copy.wait_recv()
    own = part_ref[0]
    for slot in range(1, len(found)):
        own = own + held[slot]
    total[...] = own
    sends = []
    for step in range(1, models):
        copy = pltpu.make_async_remote_copy(
            src_ref=total,
            dst_ref=others.at[step],
            send_sem=send_b.at[step],
            recv_sem=recv_b.at[step],
            device_id={"mp": lax.rem(model + step, models)},
            device_id_type=MESH,
        )
        copy.start()
        sends.append(copy)
    for copy in copies:
        copy.wait_send()
    for copy in sends:
        copy.wait_recv()
    stacked = [own] + [others[step] for step in range(1, models)]
    mean = sum(stacked[1:], stacked[0]) * (1.0 / models)
    square = jnp.zeros_like(mean)
    for one in stacked:
        square = square + (one - mean) * (one - mean)
    square = square * (1.0 / models)
    row = iota(square.shape, 0)
    force = jnp.sum(jnp.where(row < 3, square, 0.0), axis=0, keepdims=True)
    virial = jnp.sum(jnp.where((row >= 3) & (row < 12), square, 0.0), axis=0, keepdims=True)
    quarter = mean_ref.shape[1]

    def mine(value):
        result = value[:, 0:quarter]
        for part in range(1, models):
            result = jnp.where(model == part, value[:, part * quarter : (part + 1) * quarter], result)
        return result

    mean_ref[...] = mine(mean[0:3])
    force_ref[...] = mine(force)
    virial_ref[...] = mine(virial)
    for copy in sends:
        copy.wait_send()


def combine(parts, count, models, found, quarter):
    slots = len(found)
    block = parts.shape[1:]
    return pl.pallas_call(
        functools.partial(reduce_kernel, count, models, found),
        out_shape=(
            jax.ShapeDtypeStruct((3, quarter), F32),
            jax.ShapeDtypeStruct((1, quarter), F32),
            jax.ShapeDtypeStruct((1, quarter), F32),
        ),
        in_specs=[VM],
        out_specs=(VM, VM, VM),
        scratch_shapes=[
            pltpu.VMEM((slots,) + block, F32),
            pltpu.VMEM(block, F32),
            pltpu.VMEM((models,) + block, F32),
            pltpu.SemaphoreType.DMA((slots,)),
            pltpu.SemaphoreType.DMA((slots,)),
            pltpu.SemaphoreType.DMA((models,)),
            pltpu.SemaphoreType.DMA((models,)),
        ],
        compiler_params=pltpu.CompilerParams(collective_id=1, has_side_effects=True),
        name="combine",
    )(parts)


def spread_of(rows, units, width, group, flip=False):
    shape = (units, rows) if flip else (rows, units)
    row = iota(shape, 1 if flip else 0)
    unit = iota(shape, 0 if flip else 1)
    inner = row % group
    return (inner < width) & (unit == (row // group) * width + inner)


def column(mask, row_value):
    return jnp.sum(jnp.where(mask, row_value, 0.0), axis=1, keepdims=True)


def split(value, parts):
    pieces = []
    for _ in range(parts):
        piece = value.astype(BF16)
        pieces.append(piece)
        value = value - piece.astype(F32)
    return pieces


def pair_fit(weight, value):
    both = nn(weight, jnp.concatenate(split(value, 2), axis=1))
    return both[:, 0:LANES] + both[:, LANES : 2 * LANES]


def pair_nn(doubled, value):
    return nn(doubled, jnp.concatenate(split(value, 2), axis=0))


def pair_tn(weight, value):
    both = tn(weight, jnp.concatenate(split(value, 2), axis=1))
    return both[:, 0:LANES] + both[:, LANES : 2 * LANES]


def atoms_kernel(
    count, strides, found, chunk,
    pos_ref, list_ref, nb_ref,
    scale_ref, shift_ref, mid_ref, mid_bias_ref, outer_ref, out_bias_ref,
    f1_ref, f1b_ref, f2_ref, f2b_ref, f3_ref, f3b_ref, read_ref,
    part_ref,
    pscr, nscr, oh_ref, pm_ref, off_ref, inv_ref, t1_ref, t2_ref, t3_ref, h3_ref,
    m_ref, d_ref, dd_ref, dm_ref, trm_ref, tot_ref,
):
    owned = pos_ref.shape[2]
    slots = len(found)
    k_total = nb_ref.shape[0]
    half = k_total // 2
    width = scale_ref.shape[1]
    g1, g2, g3 = 32, 64, 128
    ext = oh_ref.shape[0]

    pscr[...] = jnp.zeros_like(pscr)
    for slot in range(slots):
        pscr[slot, 0:3, 0:owned] = pos_ref[slot]
    meta_row = iota((8, LANES), 0)
    lane8 = iota((8, LANES), 1)
    base = []
    for slot in range(slots):
        hi, mid, lo = split(pscr[slot], 3)
        meta = jnp.where(meta_row == 4, lane8, jnp.where(meta_row == 5, slot, 0)).astype(F32)
        base.append(
            jnp.concatenate([hi.astype(F32), mid.astype(F32), lo.astype(F32), meta], axis=0).astype(BF16)
        )
    row32 = iota((32, LANES), 0)

    def fetch(columns, source, section, side):
        wanted = list_ref[source, 2 * section + side : 2 * section + side + 1, :]
        wanted = jnp.where(wanted >= owned, wanted + (LANES - owned), wanted)
        table = columns[0] if len(columns) == 1 else jnp.concatenate(columns, axis=1)
        mask = iota((table.shape[1], LANES), 0) == wanted
        got = nn(table, hot(mask))
        sign = -1.0 if side == 0 else 1.0
        return got + jnp.where(row32 == 24 + section, sign, 0.0)

    where = {off: slot for slot, off in enumerate(found)}

    def neighbour(off, section, side):
        return (off + (-strides[section] if side == 0 else strides[section])) % count

    held = {off: [base[where[off]]] for off in found}
    needs = (
        sorted({(b * strides[1] + c * strides[2]) % count for b in (-1, 0, 1) for c in (-1, 0, 1)}),
        sorted({(c * strides[2]) % count for c in (-1, 0, 1)}),
        [0],
    )
    for section in range(3):
        fresh = {}
        for off in needs[section]:
            fresh[off] = []
            for side in range(2):
                source = neighbour(off, section, side)
                table = held[source][: 1 + 2 * section]
                fresh[off].append(fetch(table, where[source], section, side).astype(BF16))
        for off in needs[section]:
            held[off] = held[off] + fresh[off]
    mine = jnp.concatenate(held[0], axis=1).astype(F32)
    own_row = iota((8, ext), 0)
    moved = jnp.where(own_row < 3, mine[24:32], 0.0)
    place = ((mine[0:8] + mine[8:16]) + mine[16:24]) + moved
    table = jnp.concatenate([piece.astype(F32) for piece in split(place, 3)], axis=0).astype(BF16)
    source_id = mine[29:30] * float(owned) + mine[28:29]
    centre = place[:, 0:LANES]
    centre = jnp.where(lane8 < owned, centre, 0.0)
    centre = centre + pltpu.roll(centre, owned, 1)

    nscr[:, 0:owned] = nb_ref[0:half, :]
    nscr[:, owned : 2 * owned] = nb_ref[half:k_total, :]
    row_ids = iota((ext, LANES), 0)

    c1 = spread_of(g1, width, width, g1)
    r2 = spread_of(g2, 2 * width, width, g1)
    r3 = spread_of(g3, 4 * width, width, g1)
    scale_c, shift_c = column(c1, scale_ref[...]), column(c1, shift_ref[...])
    bias2_c, bias3_c = column(r2, mid_bias_ref[...]), column(r3, out_bias_ref[...])
    w2 = nn(nn(hot(r2), mid_ref[...]).astype(BF16), hot(spread_of(g1, width, width, g1, True))).astype(BF16)
    w2t = nn(nt(hot(c1), mid_ref[...]).astype(BF16), hot(spread_of(g2, 2 * width, width, g1, True))).astype(BF16)
    w3 = nn(nn(hot(r3), outer_ref[...]).astype(BF16), hot(spread_of(g2, 2 * width, width, g1, True))).astype(BF16)
    w3t = nn(nt(hot(r2), outer_ref[...]).astype(BF16), hot(spread_of(g3, 4 * width, width, g1, True))).astype(BF16)

    w2d = jnp.concatenate([w2, w2], axis=1)
    w3d = jnp.concatenate([w3, w3], axis=1)
    m_ref[...] = jnp.zeros_like(m_ref)
    tiles = chunk // LANES

    def cut(value, tile):
        return value[:, tile * LANES : (tile + 1) * LANES]

    def forward(step, carry):
        begin = pl.multiple_of(step * chunk, chunk)
        lanes = pl.ds(begin, chunk)
        masks, present = [], []
        for tile in range(tiles):
            ids = nscr[pl.ds(step * tiles + tile, 1), :]
            present.append(jnp.where(ids >= 0, 1.0, 0.0))
            ids = jnp.where(ids >= owned, ids + (LANES - owned), ids)
            masks.append(hot(row_ids == ids))
        ones = jnp.concatenate(masks, axis=1)
        oh_ref[:, lanes] = ones
        there = jnp.concatenate(present, axis=1)
        got = nn(table, ones)
        offs = (got[0:8] + got[8:16]) + got[16:24] - jnp.concatenate([centre] * tiles, axis=1)
        radius = offs[0:1] * offs[0:1] + offs[1:2] * offs[1:2] + offs[2:3] * offs[2:3] + SOFTEN
        inv = lax.rsqrt(radius)
        off_ref[:, lanes] = offs
        inv_ref[:, lanes] = inv
        pm_ref[:, lanes] = there
        t1 = jnp.tanh(scale_c * inv + shift_c)
        t1_ref[:, lanes] = t1
        t2 = jnp.tanh(pair_nn(w2d, t1) + bias2_c)
        t2_ref[:, lanes] = t2
        h2 = jnp.concatenate([t1, t1], axis=0) + t2
        t3 = jnp.tanh(pair_nn(w3d, h2) + bias3_c)
        t3_ref[:, lanes] = t3
        h3f = jnp.concatenate([h2, h2], axis=0) + t3
        h3_ref[:, lanes] = h3f
        near = there * inv
        far = near * inv
        for c in range(4):
            env = near if c == 0 else far * offs[c - 1 : c]
            add = cut(h3f, 0) * cut(env, 0)
            for tile in range(1, tiles):
                add = add + cut(h3f, tile) * cut(env, tile)
            m_ref[c] += add
        return carry

    steps = (half * LANES) // chunk
    lax.fori_loop(0, steps, forward, 0)

    for c in range(4):
        both = m_ref[c]
        m_ref[c] = (both + pltpu.roll(both, owned, 1)) * (1.0 / k_total)

    units = 4 * width
    heads = [m_ref[c, 0:AXIS, :] for c in range(4)]
    rows = [(n // width) * g1 + n % width for n in range(units)]
    for n in range(units):
        total = m_ref[0, rows[n] : rows[n] + 1, :] * heads[0]
        for c in range(1, 4):
            total = total + m_ref[c, rows[n] : rows[n] + 1, :] * heads[c]
        d_ref[n * AXIS : (n + 1) * AXIS, :] = total

    fit = f2_ref.shape[0]
    eye = iota((fit, fit), 0) == iota((fit, fit), 1)
    u1 = jnp.tanh(pair_fit(f1_ref[...], d_ref[...]) + column(eye, f1b_ref[...]))
    u2 = jnp.tanh(pair_fit(f2_ref[...], u1) + column(eye, f2b_ref[...]))
    q2 = u1 + u2
    u3 = jnp.tanh(pair_fit(f3_ref[...], q2) + column(eye, f3b_ref[...]))
    read = column(eye, read_ref[...].astype(F32))
    e3 = read * (1.0 - u3 * u3)
    back2 = (read + (pair_tn(f3_ref[...], e3)))
    e2 = back2 * (1.0 - u2 * u2)
    back1 = (back2 + (pair_tn(f2_ref[...], e2)))
    e1 = back1 * (1.0 - u1 * u1)
    dd_ref[...] = pair_tn(f1_ref[...], e1)

    dm_ref[...] = jnp.zeros_like(dm_ref)
    piled = [jnp.zeros((AXIS, LANES), F32) for _ in range(4)]
    inverse_k = 1.0 / k_total
    for n in range(units):
        piece = dd_ref[n * AXIS : (n + 1) * AXIS, :] * inverse_k
        for c in range(4):
            piled[c] = piled[c] + piece * m_ref[c, rows[n] : rows[n] + 1, :]
            dm_ref[c, rows[n] : rows[n] + 1, :] = jnp.sum(piece * heads[c], axis=0, keepdims=True)
    for c in range(4):
        dm_ref[c, 0:AXIS, :] += piled[c]

    w3tt = jnp.concatenate([w3t, w3t], axis=1)
    w2tt = jnp.concatenate([w2t, w2t], axis=1)
    tot_ref[...] = jnp.zeros_like(tot_ref)
    trm_ref[...] = jnp.zeros_like(trm_ref)

    def backward(step, middle):
        begin = pl.multiple_of(step * chunk, chunk)
        lanes = pl.ds(begin, chunk)
        offs = off_ref[:, lanes]
        inv = inv_ref[:, lanes]
        there = pm_ref[:, lanes]
        h3 = h3_ref[:, lanes]
        near = there * inv
        far = near * inv
        env = [near] + [far * offs[a : a + 1] for a in range(3)]
        pieces, denv = [], [[] for _ in range(4)]
        for tile in range(tiles):
            total = None
            for c in range(4):
                dm = dm_ref[c]
                part = cut(env[c], tile) * dm
                total = part if total is None else total + part
                denv[c].append(jnp.sum(cut(h3, tile) * dm, axis=0, keepdims=True))
            pieces.append(total)
        denv = [jnp.concatenate(one, axis=1) for one in denv]
        d3 = jnp.concatenate(pieces, axis=1)
        t3 = t3_ref[:, lanes]
        p3 = d3 * (1.0 - t3 * t3)
        d2 = (d3[0:g2] + d3[g2:g3]) + (pair_nn(w3tt, p3))
        t2 = t2_ref[:, lanes]
        p2 = d2 * (1.0 - t2 * t2)
        d1 = (d2[0:g1] + d2[g1:g2]) + (pair_nn(w2tt, p2))
        t1 = t1_ref[:, lanes]
        p1 = d1 * (1.0 - t1 * t1)
        dinv = jnp.sum(p1 * scale_c, axis=0, keepdims=True) + there * denv[0]
        mixed = denv[1] * offs[0:1] + denv[2] * offs[1:2] + denv[3] * offs[2:3]
        dinv = dinv + 2.0 * near * mixed
        pull = dinv * (inv * inv * inv)
        grads = [far * denv[a + 1] - pull * offs[a : a + 1] for a in range(3)]
        for a in range(3):
            trm_ref[a : a + 1, :] = -grads[a]
            for b in range(3):
                trm_ref[3 + 3 * a + b : 4 + 3 * a + b, :] = -(offs[a : a + 1] * grads[b])
        terms = trm_ref[...]
        high = terms.astype(BF16)
        low = (terms - high.astype(F32)).astype(BF16)
        tot_ref[...] += nt(jnp.concatenate([high, low], axis=0), oh_ref[:, lanes])
        for tile in range(tiles):
            middle = middle + cut(terms, tile)
        return middle

    middle = lax.fori_loop(0, steps, backward, jnp.zeros((16, LANES), F32))
    middle = jnp.where(iota((16, LANES), 0) < 3, middle + pltpu.roll(middle, owned, 1), 0.0)
    middle = jnp.where(iota((16, LANES), 1) < owned, middle, 0.0)
    tot_ref[0:16, 0:LANES] = tot_ref[0:16, 0:LANES] - middle
    terms = tot_ref[0:16, :] + tot_ref[16:32, :]
    high = terms.astype(BF16)
    both = jnp.concatenate([high, (terms - high.astype(F32)).astype(BF16)], axis=0)
    for slot in range(slots):
        ids = (iota((LANES, ext), 0) + slot * owned).astype(F32)
        lane_ok = iota((LANES, ext), 0) < owned
        part = nt(both, hot((ids == source_id) & lane_ok))
        part_ref[slot] = part[0:16] + part[16:32]


def atoms(pos_all, list_all, neighbours, params, count, strides, found):
    slots, _, owned = pos_all.shape
    k_total = neighbours.shape[0]
    pairs = k_total * owned
    ext = LANES + list_all.shape[1] * list_all.shape[2]
    width = params[0].shape[1]
    units = 4 * width
    tiles = max(t for t in range(1, 17) if (k_total // 2) % t == 0)
    chunk = LANES * tiles
    scratch = [
        pltpu.VMEM((slots, 8, LANES), F32),
        pltpu.VMEM((k_total // 2, LANES), jnp.int32),
        pltpu.VMEM((ext, pairs), BF16),
        pltpu.VMEM((1, pairs), F32),
        pltpu.VMEM((8, pairs), F32),
        pltpu.VMEM((1, pairs), F32),
        pltpu.VMEM((32, pairs), F32),
        pltpu.VMEM((64, pairs), F32),
        pltpu.VMEM((128, pairs), F32),
        pltpu.VMEM((128, pairs), F32),
        pltpu.VMEM((4, 128, LANES), F32),
        pltpu.VMEM((units * AXIS, LANES), F32),
        pltpu.VMEM((units * AXIS, LANES), F32),
        pltpu.VMEM((4, 128, LANES), F32),
        pltpu.VMEM((16, chunk), F32),
        pltpu.VMEM((32, ext), F32),
    ]
    args = (pos_all, list_all, neighbours) + params
    return pl.pallas_call(
        functools.partial(atoms_kernel, count, strides, found, chunk),
        out_shape=jax.ShapeDtypeStruct((slots, 16, LANES), F32),
        in_specs=[VM] * len(args),
        out_specs=VM,
        scratch_shapes=scratch,
        compiler_params=pltpu.CompilerParams(vmem_limit_bytes=67043328),
        name="atoms",
    )(*args)


def local(positions, send_lists, neighbours, *weights):
    count = lax.axis_size("space")
    models = lax.axis_size("mp")
    strides, found = dims(count)
    pos_all, list_all = share(positions, send_lists[0], count, found)
    params = tuple(one[0] if one.ndim == 3 else one for one in weights)
    parts = atoms(pos_all, list_all, neighbours, params, count, strides, found)
    quarter = positions.shape[1] // models
    mean, force, virial = combine(parts, count, models, found, quarter)
    return (
        mean.reshape(3, 1, 1, quarter),
        force.reshape(1, 1, quarter),
        virial.reshape(1, 1, quarter),
    )


def solution(mesh):
    flat, deep = P("mp", None), P("mp", None, None)
    return jax.shard_map(
        local,
        mesh=mesh,
        in_specs=(
            P(None, "space"), P("space", None, None), P(None, "space"),
            flat, flat, deep, flat, deep, flat, deep, flat, deep, flat, deep, flat, flat,
        ),
        out_specs=(P(None, "space", "mp", None), P("space", "mp", None), P("space", "mp", None)),
        check_vma=False,
    )
```

profile of v0, /device:TPU:0, one launch (start us, length us, event | category | flops | bytes accessed | tf_op | source)
XLA Modules:
  0.0 45.3 jit_solution(7010704104580331693)
XLA Ops:
  0.6 0.0 copy-start.2
  0.6 1.3 %copy.25 = s32[1,6,128]{2,1,0:T(8,128)} copy(s32[1,6,128]{2,0,1:T(1,128)} %param.17) | data formatting | bytes 6144
  1.9 0.0 copy-start.1
  1.9 0.0 copy-done.2
  1.9 0.7 %copy.19 = bf16[1,50,25]{2,1,0:T(8,128)(2,1)} copy(bf16[1,50,25]{1,2,0:T(8,128)(2,1)S(1)} %copy-done.2) | data formatting | bytes 5000 | tf_op args[5]
  2.6 0.0 copy-start
  2.6 0.0 copy-done.1
  2.6 0.7 %copy.20 = bf16[1,100,50]{2,1,0:T(8,128)(2,1)} copy(bf16[1,100,50]{1,2,0:T(8,128)(2,1)S(1)} %copy-done.1) | data formatting | bytes 20000 | tf_op args[7]
  3.4 7.8 %share.1 = (f32[8,3,64]{2,1,0:T(4,128)}, s32[8,6,128]{2,1,0:T(8,128)}) custom-call(f32[3,64]{1,0:T(4,128)} %pos_ref.1, s32[6,128]{1,0:T(8,128)} %bitcast.16), custom_call_target="tpu_custom_call" | custom-call | tf_op jit(solution)/shard_map/share/pallas_call | solution.py:89
  11.2 0.0 copy-done
  11.2 0.7 %copy.21.nb_ref = s32[96,64]{1,0:T(8,128)} copy(s32[96,64]{0,1:T(8,128)S(1)} %copy-done) | data formatting | bytes 49152 | tf_op args[2]
  11.9 18.6 %atoms.1.part_ref = f32[8,16,128]{2,1,0:T(8,128)} custom-call(f32[8,3,64]{2,1,0:T(4,128)} %get-tuple-element.8.pos_ref, s32[8,6,128]{2,1,0:T(8,128)} %get-tuple-element.9.list_ref, s32[96,64]{1,0:T(8,128)} %copy.21.nb_ref, f32[1,25]{1,0:T(1,128)} %scale_ref.1, f32[1,25]{1,0:T(1,128)} %shift_ref.1, bf16[50,25]{1,0:T(8,128)(2,1)} %bitcast.15, ...), custom_call_target="tpu_custom_call" | custom-call | tf_op jit(solution)/shard_map/atoms/pallas_call | solution.py:503
  30.5 11.9 %combine.1 = (f32[3,16]{1,0:T(4,128)}, f32[1,16]{1,0:T(1,128)}, f32[1,16]{1,0:T(1,128)}) custom-call(f32[8,16,128]{2,1,0:T(8,128)} %atoms.1.part_ref), custom_call_target="tpu_custom_call" | custom-call | tf_op jit(solution)/shard_map/combine/pallas_call | solution.py:180
  42.4 0.0 copy-start.3
  42.4 0.7 %copy-done.3 = f32[3,16]{1,0:T(4,128)S(1)} copy-done((f32[3,16]{1,0:T(4,128)S(1)}, f32[3,16]{1,0:T(4,128)}, u32[]{:S(2)}) %copy-start.3) | copy-done | bytes 216
  43.0 0.6 %copy.22 = f32[3,1,1,16]{3,2,1,0:T(1,128)} copy(f32[3,1,1,16]{3,0,2,1:T(4,128)S(1)} %bitcast.17) | data formatting | bytes 384
  43.6 0.0 copy-start.5
  43.6 0.6 %copy-done.5 = f32[1,16]{1,0:T(1,128)S(1)} copy-done((f32[1,16]{1,0:T(1,128)S(1)}, f32[1,16]{1,0:T(1,128)}, u32[]{:S(2)}) %copy-start.5) | copy-done | bytes 88
  44.2 0.0 copy-start.4
  44.2 0.5 %copy.28 = f32[1,1,16]{2,1,0:T(1,128)} copy(f32[1,1,16]{2,1,0:T(1,128)S(1)} %bitcast.19) | data formatting | bytes 128
  44.7 0.1 copy-done.4
  44.8 0.5 %copy.29 = f32[1,1,16]{2,1,0:T(1,128)} copy(f32[1,1,16]{2,1,0:T(1,128)S(1)} %bitcast.18) | data formatting | bytes 128
Async XLA Ops:
  0.6 1.3 %copy-start.2 = (bf16[1,50,25]{1,2,0:T(8,128)(2,1)S(1)}, bf16[1,50,25]{1,2,0:T(8,128)(2,1)}, u32[]{:S(2)}) copy-start(bf16[1,50,25]{1,2,0:T(8,128)(2,1)} %param.21) | copy-start | bytes 7504
  1.9 0.7 %copy-start.1 = (bf16[1,100,50]{1,2,0:T(8,128)(2,1)S(1)}, bf16[1,100,50]{1,2,0:T(8,128)(2,1)}, u32[]{:S(2)}) copy-start(bf16[1,100,50]{1,2,0:T(8,128)(2,1)} %param.23) | copy-start | bytes 30004
  2.6 8.6 %copy-start = (s32[96,64]{0,1:T(8,128)S(1)}, s32[96,64]{0,1:T(8,128)}, u32[]{:S(2)}) copy-start(s32[96,64]{0,1:T(8,128)} %param.18) | copy-start | bytes 73732
  42.4 0.7 %copy-start.3 = (f32[3,16]{1,0:T(4,128)S(1)}, f32[3,16]{1,0:T(4,128)}, u32[]{:S(2)}) copy-start(f32[3,16]{1,0:T(4,128)} %get-tuple-element.10) | copy-start | bytes 580
  43.6 0.6 %copy-start.5 = (f32[1,16]{1,0:T(1,128)S(1)}, f32[1,16]{1,0:T(1,128)}, u32[]{:S(2)}) copy-start(f32[1,16]{1,0:T(1,128)} %get-tuple-element.11) | copy-start | bytes 196
  44.2 0.6 %copy-start.4 = (f32[1,16]{1,0:T(1,128)S(1)}, f32[1,16]{1,0:T(1,128)}, u32[]{:S(2)}) copy-start(f32[1,16]{1,0:T(1,128)} %get-tuple-element.12) | copy-start | bytes 196
where the time goes:
time: 45.7 us; the launch traced here: 45.3 us
  Pallas kernels  38.3 us (84%)
  local copies, waits for them, and re-layouts  6.37 us (14%)
  between operations  0.68 us (1%)
    pallas_call x1, Pallas kernels, atoms(): pl.pallas_call(functools.partial(atoms_kernel, count, strides, found, chu...  18.6 us
    pallas_call x1, Pallas kernels, combine(): pl.pallas_call(functools.partial(reduce_kernel, count, models, found), ou...  11.9 us
    pallas_call x1, Pallas kernels, share(): pl.pallas_call(functools.partial(share_kernel, count, found), out_shape=(...  7.84 us
    unnamed x19, local copies, waits for them, and re-layouts  6.37 us

commit v1 on v0

v1 whole, which is shorter than its diff:
```python
import functools
import math

import jax
import jax.numpy as jnp
from jax import lax
from jax.experimental import pallas as pl
from jax.experimental.pallas import tpu as pltpu
from jax.sharding import PartitionSpec as P

AXIS = 16
SOFTEN = 0.04
LANES = 128
ROWS = 2
ONE = 20.0
MESH = pl.DeviceIdType.MESH
F32 = jnp.float32
BF16 = jnp.bfloat16
I32 = jnp.int32
ANY = pl.BlockSpec(memory_space=pl.ANY)
VM = pl.BlockSpec(memory_space=pltpu.VMEM)


def dims(space_count):
    grid_y = min(4, max(2, space_count // 16))
    strides = (grid_y * grid_y, grid_y, 1)
    span = (-1, 0, 1)
    found = sorted(
        {
            (a * strides[0] + b * strides[1] + c * strides[2]) % space_count
            for a in span
            for b in span
            for c in span
        }
    )
    return strides, found


def nn(a, b):
    return jnp.dot(a, b, preferred_element_type=F32)


def nt(a, b):
    return lax.dot_general(a, b, (((1,), (1,)), ((), ())), preferred_element_type=F32)


def tn(a, b):
    return lax.dot_general(a, b, (((0,), (0,)), ((), ())), preferred_element_type=F32)


def iota(shape, dim):
    return lax.broadcasted_iota(I32, shape, dim)


def hot(mask):
    return jnp.where(mask, 1.0, 0.0).astype(BF16)


def spread_of(rows, units, width, group, flip=False):
    shape = (units, rows) if flip else (rows, units)
    row = iota(shape, 1 if flip else 0)
    unit = iota(shape, 0 if flip else 1)
    inner = row % group
    return (inner < width) & (unit == (row // group) * width + inner)


def column(mask, row_value):
    return jnp.sum(jnp.where(mask, row_value, 0.0), axis=1, keepdims=True)


def rounded(value):
    return value.astype(BF16).astype(F32)


def split(value, parts):
    pieces = []
    for _ in range(parts):
        piece = value.astype(BF16)
        pieces.append(piece)
        value = value - piece.astype(F32)
    return pieces


def both(value):
    return jnp.concatenate(split(value, 2), axis=0)


def lookup(row, lane):
    return jnp.take_along_axis(
        jnp.broadcast_to(row, lane.shape), lane, axis=1, mode="promise_in_bounds"
    )


def with_bias(weight, bias, width):
    col = iota(weight.shape, 1)
    for place, piece in enumerate(split(bias, 3)):
        weight = jnp.where(col == width + place, piece.astype(F32), weight)
    return weight.astype(BF16)


def kernel(
    count, models, strides, found, sizes,
    pos_in, list_in, nb_in,
    scale_in, shift_in, mid_in, midb_in, outer_in, outb_in,
    f1_in, f1b_in, f2_in, f2b_in, f3_in, f3b_in, read_in,
    mean_ref, force_ref, virial_ref,
    pos_all, list_all, nb_ref, scale_ref, shift_ref, mid_ref, midb_ref, outer_ref, outb_ref,
    f1_ref, f1b_ref, f2_ref, f2b_ref, f3_ref, f3b_ref, read_ref,
    nscr, ptab, code_ref, f1p_ref, sel_ref, oh_ref, em_ref,
    w2_ref, w3_ref, a2_ref, a3_ref,
    off_ref, inv_ref, there_ref, id_ref, cen_ref, e4h_ref, e4l_ref,
    t1_ref, s2_ref, s3_ref, h3_ref, ms_ref, bm_ref, d_ref, dd_ref, y_ref, dms_ref,
    de4_ref, di_ref, th_ref, tl_ref, lhs_ref, part_ref, held, total, others,
    local_sem, send_a, recv_a, send_b, recv_b, send_c, recv_c, send_d, recv_d,
):
    owned, k_total, width, fit = sizes
    slots = len(found)
    group = LANES // math.gcd(k_total, LANES)
    tiles = group * k_total // LANES
    rows = owned // group
    chunks = rows // ROWS
    span = ROWS * tiles * LANES
    units = 4 * width
    g1, g2, g3 = 32, 64, 128
    pairs = ROWS * group * 4
    masks_count = (slots * owned + LANES - 1) // LANES
    me = lax.axis_index("space")
    model = lax.axis_index("mp")

    barrier = pltpu.get_barrier_semaphore()
    for off in found[1:]:
        pl.semaphore_signal(
            barrier, inc=1, device_id={"space": lax.rem(me + off, count)}, device_id_type=MESH
        )
    for step in range(1, models):
        pl.semaphore_signal(
            barrier, inc=1, device_id={"mp": lax.rem(model + step, models)}, device_id_type=MESH
        )
    moves = [
        (pos_in, pos_all.at[0]), (list_in, list_all.at[0]), (nb_in, nb_ref),
        (scale_in, scale_ref), (shift_in, shift_ref), (mid_in.at[0], mid_ref), (midb_in, midb_ref),
        (outer_in.at[0], outer_ref), (outb_in, outb_ref), (f1_in.at[0], f1_ref), (f1b_in, f1b_ref),
        (f2_in.at[0], f2_ref), (f2b_in, f2b_ref), (f3_in.at[0], f3_ref), (f3b_in, f3b_ref),
        (read_in, read_ref),
    ]
    fetched = []
    for place, (src, dst) in enumerate(moves):
        copy = pltpu.make_async_copy(src, dst, local_sem.at[place])
        copy.start()
        fetched.append(copy)
    em_ref[...] = jnp.zeros_like(em_ref)
    th_ref[...] = jnp.zeros_like(th_ref)
    tl_ref[...] = jnp.zeros_like(tl_ref)
    nscr[...] = jnp.zeros_like(nscr)
    ptab[...] = jnp.zeros_like(ptab)
    for copy in fetched[:9]:
        copy.wait()

    c1 = spread_of(g1, width, width, g1)
    r2 = spread_of(g2, 2 * width, width, g1)
    r3 = spread_of(g3, 4 * width, width, g1)
    scale_c, shift_c = column(c1, scale_ref[...]), column(c1, shift_ref[...])
    unit_row = iota((g1, 1), 0)
    shift_c = jnp.where((unit_row >= width) & (unit_row < width + 3), ONE, shift_c)
    bias2_c, bias3_c = column(r2, midb_ref[...]), column(r3, outb_ref[...])
    wide1 = hot(spread_of(g1, width, width, g1, True))
    wide2 = hot(spread_of(g2, 2 * width, width, g1, True))
    wide3 = hot(spread_of(g3, 4 * width, width, g1, True))
    mid_t, outer_t = mid_ref[...], outer_ref[...]
    w2 = nn(nt(hot(r2), mid_t).astype(BF16), wide1)
    w2t = nn(nn(hot(c1), mid_t).astype(BF16), wide2)
    w3 = nn(nt(hot(r3), outer_t).astype(BF16), wide2)
    w3t = nn(nn(hot(r2), outer_t).astype(BF16), wide3)
    w2_ref[...] = with_bias(w2, bias2_c, width)
    w3_ref[...] = with_bias(w3, bias3_c, width)
    fold2 = hot(iota((g1, g2), 1) % g1 == iota((g1, g2), 0))
    fold3 = hot(iota((g2, g3), 1) % g2 == iota((g2, g3), 0))
    a2_ref[...] = jnp.concatenate([w2t.astype(BF16), fold2], axis=1)
    a3_ref[...] = jnp.concatenate([w3t.astype(BF16), fold3], axis=1)

    pl.semaphore_wait(barrier, len(found) - 1 + models - 1)
    shares = []
    for slot, off in enumerate(found):
        if off == 0:
            continue
        peer = lax.rem(me + count - off, count)
        for ref, send, recv in ((pos_all, send_a, recv_a), (list_all, send_b, recv_b)):
            copy = pltpu.make_async_remote_copy(
                src_ref=ref.at[0],
                dst_ref=ref.at[slot],
                send_sem=send.at[slot],
                recv_sem=recv.at[slot],
                device_id={"space": peer},
                device_id_type=MESH,
            )
            copy.start()
            shares.append(copy)

    nscr[:, 0:k_total] = nb_ref[...]
    lane = iota((rows, LANES), 1)
    own_row = iota((rows, LANES), 0)
    turned = [
        pltpu.roll(nscr[a * rows : (a + 1) * rows, :], (k_total * a) % LANES, 1) if (k_total * a) % LANES
        else nscr[a * rows : (a + 1) * rows, :]
        for a in range(group)
    ]
    member = []
    wanted = []
    for tile in range(tiles):
        place = lane + tile * LANES
        which = jnp.zeros_like(lane)
        for a in range(1, group):
            which = which + jnp.where(place >= a * k_total, 1, 0)
        member.append(which)
        value = turned[0]
        for a in range(1, group):
            value = jnp.where(which == a, turned[a], value)
        wanted.append(value)

    own_pos = jnp.concatenate([pos_all[0], jnp.zeros((3, LANES - owned), F32)], axis=1)
    for tile in range(tiles):
        at = member[tile] * rows + own_row
        for c in range(3):
            cen_ref[c, :, tile * LANES : (tile + 1) * LANES] = lookup(own_pos[c : c + 1], at)

    fetched[9].wait()

    def order(step, carry):
        source = iota((units * AXIS, 2 * LANES), 0)
        col = iota((units * AXIS, 2 * LANES), 1)
        unit = source >> 4
        padded = unit
        for a in range(1, 4):
            padded = padded + jnp.where(unit >= a * width, g1 - width, 0)
        target = padded + LANES * ((source & (AXIS - 1)) - 2 * step)
        f1p_ref[:, pl.ds(pl.multiple_of(step * 2 * LANES, 2 * LANES), 2 * LANES)] = nn(
            f1_ref[...], hot(target == col)
        ).astype(BF16)
        return carry

    lax.fori_loop(0, AXIS // 2, order, 0)
    sel_ref[...] = hot((iota(sel_ref.shape, 0) >> 7) == iota(sel_ref.shape, 1))

    def own_hot(step, carry):
        for inner in range(ROWS):
            r = step * ROWS + inner
            for tile in range(tiles):
                at = pl.multiple_of((r * tiles + tile) * LANES, LANES)
                which = member[tile][0:1] * rows + r
                oh_ref[LANES : 2 * LANES, pl.ds(at, LANES)] = hot(iota((LANES, LANES), 0) == which)
        return carry

    lax.fori_loop(0, chunks, own_hot, 0)
    for copy in fetched[10:]:
        copy.wait()

    for copy in shares:
        copy.wait_recv()

    base = sum(1 << (16 + 2 * s) for s in range(3))
    where = {off: slot for slot, off in enumerate(found)}

    def neighbour(off, section, side):
        return (off + (-strides[section] if side == 0 else strides[section])) % count

    needs = (
        sorted({(b * strides[1] + c * strides[2]) % count for b in (-1, 0, 1) for c in (-1, 0, 1)}),
        sorted({(c * strides[2]) % count for c in (-1, 0, 1)}),
        [0],
    )
    place = {}
    for section in range(3):
        for off in needs[section]:
            for side in range(2):
                place[(off, 2 * section + side)] = len(place)
    for section in range(3):
        todo = [(off, side) for off in needs[section] for side in range(2)]
        if section == 0:
            for off, side in todo:
                source = neighbour(off, section, side)
                slot = where[source]
                shift = (-1 if side == 0 else 1) << (16 + 2 * section)
                at = place[(off, side)]
                code_ref[at : at + 1, :] = list_all[slot, side] + (slot * owned + base + shift)
            continue
        names, bases, tables = [], [], [[] for _ in range(2 * section)]
        for off, side in todo:
            source = neighbour(off, section, side)
            slot = where[source]
            names.append(list_all[slot, 2 * section + side])
            shift = (-1 if side == 0 else 1) << (16 + 2 * section)
            bases.append((slot * owned + base, shift))
            for block in range(2 * section):
                at = place[(source, block)]
                tables[block].append(code_ref[at : at + 1, :])
        for index, (off, side) in enumerate(todo):
            name = jnp.broadcast_to(names[index], (8, LANES))
            moved = jnp.where(name >= owned, name + (LANES - owned), name)
            row = moved >> 7
            spot = moved & (LANES - 1)
            result = name + bases[index][0]
            for block in range(2 * section):
                result = jnp.where(row == block + 1, lookup(tables[block][index], spot), result)
            at = place[(off, 2 * section + side)]
            code_ref[at : at + 1, :] = result[0:1] + bases[index][1]

    for slot in range(slots):
        at = (slot * owned) % LANES
        ptab[(slot * owned) // LANES, 0:3, at : at + owned] = pos_all[slot]

    for tile in range(tiles):
        cut = slice(tile * LANES, (tile + 1) * LANES)
        j = wanted[tile]
        there = jnp.where(j >= 0, 1.0, 0.0)
        moved = jnp.where(j >= owned, j + (LANES - owned), j)
        row = moved >> 7
        spot = moved & (LANES - 1)
        code = j + base
        for block in range(6):
            at = place[(0, block)]
            code = jnp.where(row == block + 1, lookup(code_ref[at : at + 1, :], spot), code)
        code = jnp.where(j >= 0, code, base)
        ident = code & 65535
        id_ref[tile] = ident
        prow = ident >> 7
        spot = ident & (LANES - 1)
        offs = []
        for c in range(3):
            value = lookup(ptab[0, c : c + 1, :], spot)
            for part in range(1, ptab.shape[0]):
                value = jnp.where(prow == part, lookup(ptab[part, c : c + 1, :], spot), value)
            moved_by = (((code >> (16 + 2 * c)) & 3) - 1).astype(F32)
            offs.append((value + moved_by) - cen_ref[c, :, cut])
        radius = offs[0] * offs[0] + offs[1] * offs[1] + offs[2] * offs[2] + SOFTEN
        inv = lax.rsqrt(radius)
        near = there * inv
        far = near * inv
        there_ref[:, cut] = there
        inv_ref[tile] = inv
        for c in range(4):
            env = near if c == 0 else far * offs[c - 1]
            high = rounded(env)
            low = env - high
            if c > 0:
                off_ref[c - 1, :, cut] = offs[c - 1]
            for twice in range(2):
                e4h_ref[tile, pl.ds(4 * twice + c, rows, stride=8), :] = high
                e4l_ref[tile, pl.ds(4 * twice + c, rows, stride=8), :] = low

    sub8 = iota((8, LANES), 0) >> 2
    picks = [
        [member[tile][0:8] == 2 * v + sub8 for v in range(group // 2)] for tile in range(tiles)
    ]
    w2, w3 = w2_ref[...], w3_ref[...]

    def forward(ch, carry):
        lanes = pl.ds(pl.multiple_of(ch * span, span), span)
        inv = jnp.concatenate(
            [inv_ref[tile, pl.ds(ch * ROWS + inner, 1), :] for inner in range(ROWS) for tile in range(tiles)],
            axis=1,
        )
        t1 = jnp.tanh(scale_c * inv + shift_c)
        t1_ref[:, lanes] = t1
        h1 = t1.astype(BF16)
        h1f = h1.astype(F32)
        u2 = jnp.tanh(nn(w2, h1))
        h2 = (jnp.concatenate([h1f, h1f], axis=0) + u2).astype(BF16)
        s2_ref[:, lanes] = (1.0 - u2 * u2).astype(BF16)
        u3 = jnp.tanh(nn(w3, h2))
        h2f = h2.astype(F32)
        h3 = (jnp.concatenate([h2f, h2f], axis=0) + u3).astype(BF16)
        s3_ref[:, lanes] = (1.0 - u3 * u3).astype(BF16)
        h3_ref[:, lanes] = h3
        for inner in range(ROWS):
            r = ch * ROWS + inner
            for tile in range(tiles):
                cut = slice(tile * LANES, (tile + 1) * LANES)
                at = pl.ds(pl.multiple_of((r * tiles + tile) * LANES, LANES), LANES)
                for part, ref in enumerate((e4h_ref, e4l_ref)):
                    value = ref[tile, pl.ds(pl.multiple_of(r * 8, 8), 8), :]
                    block = jnp.concatenate(
                        [jnp.where(pick, value, 0.0) for pick in picks[tile]], axis=0
                    ).astype(BF16)
                    size = 4 * group
                    em_ref[part * pairs + inner * size : part * pairs + (inner + 1) * size, at] = block
                    if part == 0:
                        em_ref[2 * pairs + inner * size : 2 * pairs + (inner + 1) * size, at] = block
                ident = id_ref[tile, pl.ds(r, 1), :] & (LANES - 1)
                oh_ref[0:LANES, at] = hot(iota((LANES, LANES), 0) == ident)
        moment = nt(em_ref[0 : 2 * pairs, lanes], h3)
        ms_ref[pl.ds(pl.multiple_of(ch * pairs, pairs), pairs), :] = (
            moment[0:pairs] + moment[pairs : 2 * pairs]
        )
        return carry

    lax.fori_loop(0, chunks, forward, 0)

    inverse_k = 1.0 / k_total
    mt = [ms_ref[pl.ds(c, owned, stride=4), :] * inverse_k for c in range(4)]
    for p in range(AXIS):
        total_p = None
        for c in range(4):
            wide = jnp.broadcast_to(mt[c][:, p : p + 1], (owned, LANES))
            bm_ref[c * AXIS + p] = wide
            part = mt[c] * wide
            total_p = part if total_p is None else total_p + part
        d_ref[:, p * LANES : (p + 1) * LANES] = total_p.astype(BF16)

    u1 = jnp.tanh(nt(d_ref[...], f1p_ref[...]) + f1b_ref[...])
    q1 = u1.astype(BF16)
    u2 = jnp.tanh(nt(q1, f2_ref[...]) + f2b_ref[...])
    q2 = (q1.astype(F32) + u2).astype(BF16)
    u3 = jnp.tanh(nt(q2, f3_ref[...]) + f3b_ref[...])
    read = read_ref[...].astype(F32)

    def back(value, weight):
        pair = nn(both(value), weight)
        return rounded(pair[0:owned] + pair[owned : 2 * owned])

    b2 = rounded(read + back(read * ((1.0 + u3) * (1.0 - u3)), f3_ref[...]))
    b1 = rounded(b2 + back(b2 * ((1.0 + u2) * (1.0 - u2)), f2_ref[...]))
    dd_ref[...] = back(b1 * ((1.0 + u1) * (1.0 - u1)), f1p_ref[...])

    sums = [None] * 4
    for p in range(AXIS):
        dd = dd_ref[:, p * LANES : (p + 1) * LANES]
        for c in range(4):
            part = dd * bm_ref[c * AXIS + p]
            sums[c] = part if sums[c] is None else sums[c] + part
            y_ref[c * owned : (c + 1) * owned, p * LANES : (p + 1) * LANES] = (dd * mt[c]).astype(BF16)
    piled = nn(y_ref[...], sel_ref[...])
    for c in range(4):
        dms_ref[pl.ds(c, owned, stride=4), :] = (sums[c] + piled[c * owned : (c + 1) * owned]) * inverse_k

    a2, a3 = a2_ref[...], a3_ref[...]

    def backward(ch, carry):
        lanes = pl.ds(pl.multiple_of(ch * span, span), span)
        high, low = split(dms_ref[pl.ds(pl.multiple_of(ch * pairs, pairs), pairs), :], 2)
        h3 = h3_ref[:, lanes]
        d3 = tn(jnp.concatenate([high, high, low], axis=0), em_ref[:, lanes]).astype(BF16)
        p3 = d3 * s3_ref[:, lanes]
        d2 = nn(a3, jnp.concatenate([p3, d3], axis=0)).astype(BF16)
        p2 = d2 * s2_ref[:, lanes]
        d1 = nn(a2, jnp.concatenate([p2, d2], axis=0))
        t1 = t1_ref[:, lanes]
        p1 = jnp.sum(d1 * (1.0 - t1 * t1) * scale_c, axis=0, keepdims=True)
        denv = nn(jnp.concatenate([high, low], axis=0), h3)
        denv = denv[0:pairs] + denv[pairs : 2 * pairs]
        for inner in range(ROWS):
            r = ch * ROWS + inner
            for tile in range(tiles):
                at = (inner * tiles + tile) * LANES
                di_ref[tile, pl.ds(r, 1), :] = p1[:, at : at + LANES]
                value = None
                for v, pick in enumerate(picks[tile]):
                    first = inner * 4 * group + 8 * v
                    part = jnp.where(pick, denv[first : first + 8, at : at + LANES], 0.0)
                    value = part if value is None else value + part
                value = value + pltpu.roll(value, 4, 0)
                de4_ref[tile, pl.ds(pl.multiple_of(r * 8, 8), 8), :] = value
        return carry

    lax.fori_loop(0, chunks, backward, 0)

    for tile in range(tiles):
        cut = slice(tile * LANES, (tile + 1) * LANES)
        offs = [off_ref[a, :, cut] for a in range(3)]
        inv, there = inv_ref[tile], there_ref[:, cut]
        denv = [de4_ref[tile, pl.ds(c, rows, stride=8), :] for c in range(4)]
        near = there * inv
        far = near * inv
        mixed = denv[1] * offs[0] + denv[2] * offs[1] + denv[3] * offs[2]
        dinv = di_ref[tile] + there * denv[0] + 2.0 * near * mixed
        pull = dinv * (inv * inv * inv)
        grads = [far * denv[a + 1] - pull * offs[a] for a in range(3)]
        terms = [-one for one in grads]
        terms += [-(offs[a] * grads[b]) for a in range(3) for b in range(3)]
        for at, term in enumerate(terms):
            high = rounded(term)
            th_ref[tile, pl.ds(at, rows, stride=16), :] = high
            tl_ref[tile, pl.ds(at, rows, stride=16), :] = term - high

    def scatter(ch, sums):
        for inner in range(ROWS):
            r = ch * ROWS + inner
            for tile in range(tiles):
                cut = slice(tile * LANES, (tile + 1) * LANES)
                at = slice((inner * tiles + tile) * LANES, (inner * tiles + tile + 1) * LANES)
                band = jnp.broadcast_to(id_ref[tile, pl.ds(r, 1), :] >> 7, (16, LANES))
                for part, ref in enumerate((th_ref, tl_ref)):
                    value = ref[tile, pl.ds(pl.multiple_of(r * 16, 16), 16), :]
                    for m in range(masks_count):
                        first = (2 * m + part) * 16
                        lhs_ref[first : first + 16, at] = jnp.where(band == m, value, 0.0).astype(BF16)
        lanes = pl.ds(pl.multiple_of(ch * span, span), span)
        return sums + nt(lhs_ref[...], oh_ref[:, lanes])

    sums = lax.fori_loop(0, chunks, scatter, jnp.zeros((32 * masks_count, 2 * LANES), F32))
    centre = jnp.zeros((16, LANES), F32)
    for m in range(masks_count):
        upper = sums[32 * m : 32 * m + 16]
        lower = sums[32 * m + 16 : 32 * m + 32]
        whole = upper + lower
        part_ref[m] = whole[:, 0:LANES]
        centre = centre + whole[:, LANES : 2 * LANES]
    centre = jnp.where(iota((16, LANES), 0) < 3, centre, 0.0)
    mine = part_ref[0] - centre

    sent = []
    for slot, off in enumerate(found):
        if off == 0:
            continue
        copy = pltpu.make_async_remote_copy(
            src_ref=part_ref.at[(slot * owned) // LANES],
            dst_ref=held.at[slot],
            send_sem=send_c.at[slot],
            recv_sem=recv_c.at[slot],
            device_id={"space": lax.rem(me + off, count)},
            device_id_type=MESH,
        )
        copy.start()
        sent.append(copy)
    for copy in sent:
        copy.wait_recv()
    per = LANES // owned
    lots = [None] * per
    for slot in range(slots):
        value = mine if slot == 0 else held[slot]
        lots[slot % per] = value if lots[slot % per] is None else lots[slot % per] + value
    own = lots[0]
    for at in range(1, per):
        own = own + pltpu.roll(lots[at], LANES - at * owned, 1)
    total[...] = own
    last = []
    for step in range(1, models):
        copy = pltpu.make_async_remote_copy(
            src_ref=total,
            dst_ref=others.at[step],
            send_sem=send_d.at[step],
            recv_sem=recv_d.at[step],
            device_id={"mp": lax.rem(model + step, models)},
            device_id_type=MESH,
        )
        copy.start()
        last.append(copy)
    for copy in shares + sent:
        copy.wait_send()
    for copy in last:
        copy.wait_recv()
    stacked = [own] + [others[step] for step in range(1, models)]
    mean = sum(stacked[1:], stacked[0]) * (1.0 / models)
    square = jnp.zeros_like(mean)
    for one in stacked:
        square = square + (one - mean) * (one - mean)
    square = square * (1.0 / models)
    row = iota(square.shape, 0)
    force = jnp.sum(jnp.where(row < 3, square, 0.0), axis=0, keepdims=True)
    virial = jnp.sum(jnp.where((row >= 3) & (row < 12), square, 0.0), axis=0, keepdims=True)
    quarter = owned // models

    def pick_mine(value):
        result = value[:, 0:quarter]
        for part in range(1, models):
            result = jnp.where(model == part, value[:, part * quarter : (part + 1) * quarter], result)
        return result

    means = pick_mine(mean[0:3])
    for c in range(3):
        mean_ref[c, 0] = means[c : c + 1]
    force_ref[0] = pick_mine(force)
    virial_ref[0] = pick_mine(virial)
    for copy in last:
        copy.wait_send()


def local(positions, send_lists, neighbours, *weights):
    count = lax.axis_size("space")
    models = lax.axis_size("mp")
    strides, found = dims(count)
    slots = len(found)
    owned = positions.shape[1]
    k_total = neighbours.shape[0]
    width = weights[0].shape[1]
    units = 4 * width
    quarter = owned // models
    blocks, cap = send_lists.shape[1:]
    lists = jnp.transpose(send_lists, (1, 0, 2))
    named = neighbours.T
    scale, shift, mid, midb, outer, outb, f1, f1b, f2, f2b, f3, f3b, read = weights
    mid = jnp.swapaxes(mid, 1, 2)
    outer = jnp.swapaxes(outer, 1, 2)
    fit = f1.shape[1]
    group = LANES // math.gcd(k_total, LANES)
    rows = owned // group
    all_pairs = owned * k_total
    row_lanes = group * k_total
    tiles = row_lanes // LANES
    pairs = ROWS * group * 4
    bands = (slots * owned + LANES - 1) // LANES
    span = ROWS * row_lanes
    args = (positions, lists, named, scale, shift, mid, midb, outer, outb, f1, f1b, f2, f2b, f3, f3b, read)

    def vm(shape, dtype=F32):
        return pltpu.VMEM(shape, dtype)

    scratch = [
        vm((slots, 3, owned)), vm((slots, blocks, 1, cap), I32), vm((owned, k_total), I32),
        vm((1, width)), vm((1, width)), vm((width, 2 * width), BF16), vm((1, 2 * width)),
        vm((2 * width, 4 * width), BF16), vm((1, 4 * width)),
        vm((fit, units * AXIS), BF16), vm((1, fit)), vm((fit, fit), BF16), vm((1, fit)),
        vm((fit, fit), BF16), vm((1, fit)), vm((1, fit), BF16),
        vm((owned, LANES), I32), vm((bands, 8, LANES)), vm((64, LANES), I32),
        vm((fit, AXIS * LANES), BF16), vm((AXIS * LANES, LANES), BF16),
        vm((2 * LANES, all_pairs), BF16), vm((3 * pairs, all_pairs), BF16),
        vm((64, 32), BF16), vm((128, 64), BF16), vm((32, 128), BF16), vm((64, 256), BF16),
        vm((3, rows, row_lanes)), vm((tiles, rows, LANES)), vm((rows, row_lanes)),
        vm((tiles, rows, LANES), I32), vm((3, rows, row_lanes)),
        vm((tiles, 8 * rows, LANES)), vm((tiles, 8 * rows, LANES)),
        vm((32, all_pairs)), vm((64, all_pairs), BF16), vm((128, all_pairs), BF16),
        vm((128, all_pairs), BF16), vm((4 * owned, LANES)), vm((4 * AXIS, owned, LANES)),
        vm((owned, AXIS * LANES), BF16), vm((owned, AXIS * LANES)),
        vm((4 * owned, AXIS * LANES), BF16), vm((4 * owned, LANES)),
        vm((tiles, 8 * rows, LANES)), vm((tiles, rows, LANES)),
        vm((tiles, 16 * rows, LANES)), vm((tiles, 16 * rows, LANES)), vm((32 * bands, span), BF16),
        vm((bands, 16, LANES)), vm((slots, 16, LANES)), vm((16, LANES)), vm((models, 16, LANES)),
        pltpu.SemaphoreType.DMA((len(args),)),
    ]
    scratch += [pltpu.SemaphoreType.DMA((slots,))] * 6 + [pltpu.SemaphoreType.DMA((models,))] * 2
    return pl.pallas_call(
        functools.partial(
            kernel, count, models, strides, found, (owned, k_total, width, fit)
        ),
        out_shape=(
            jax.ShapeDtypeStruct((3, 1, 1, quarter), F32),
            jax.ShapeDtypeStruct((1, 1, quarter), F32),
            jax.ShapeDtypeStruct((1, 1, quarter), F32),
        ),
        in_specs=[ANY] * len(args),
        out_specs=(VM, VM, VM),
        scratch_shapes=scratch,
        compiler_params=pltpu.CompilerParams(
            collective_id=0, has_side_effects=True, vmem_limit_bytes=60000000
        ),
        name="forces",
    )(*args)


def solution(mesh):
    flat, deep = P("mp", None), P("mp", None, None)
    return jax.shard_map(
        local,
        mesh=mesh,
        in_specs=(
            P(None, "space"), P("space", None, None), P(None, "space"),
            flat, flat, deep, flat, deep, flat, deep, flat, deep, flat, deep, flat, flat,
        ),
        out_specs=(P(None, "space", "mp", None), P("space", "mp", None), P("space", "mp", None)),
        check_vma=False,
    )
```

time: 45.7 us -> 38.7 us (0.85)
  local copies, waits for them, and re-layouts: 6.37 us -> 2.34 us
  Pallas kernels: 38.3 us -> 35.5 us
    unnamed x19 -> x9, local copies, waits for them, and re-layouts: 6.37 us -> 2.34 us
    pallas_call x3 -> x1, Pallas kernels: 38.3 us -> 35.5 us  [local(): pl.pallas_call(functools.partial(kernel, count, models, strides, found, (...]
where the time goes in v1:
time: 38.7 us; the launch traced here: 38.5 us
  Pallas kernels  35.5 us (92%)
  local copies, waits for them, and re-layouts  2.34 us (6%)
  between operations  0.66 us (2%)
    pallas_call x1, Pallas kernels, local(): pl.pallas_call(functools.partial(kernel, count, models, strides, found, (...  35.5 us
    unnamed x9, local copies, waits for them, and re-layouts  2.34 us

profile of v1, /device:TPU:0, one launch (start us, length us, event | category | flops | bytes accessed | tf_op | source)
XLA Modules:
  0.0 38.5 jit_solution(10355171244261605369)
XLA Ops:
  0.6 35.5 %forces.1 = (f32[3,1,1,16]{3,2,1,0:T(1,128)}, f32[1,1,16]{2,1,0:T(1,128)}, f32[1,1,16]{2,1,0:T(1,128)}) custom-call(f32[3,64]{1,0:T(4,128)} %pos_in.1, s32[6,1,128]{2,1,0:T(1,128)} %bitcast.7, s32[64,96]{1,0:T(8,128)} %bitcast.4, f32[1,25]{1,0:T(1,128)} %scale_in.1, f32[1,25]{1,0:T(1,128)} %shift_in.1, bf16[1,25,50]{2,1,0:T(8,128)(2,1)} %bitcast.6, ...), custom_call_target="tpu_custom_call" | custom-call | tf_op jit(solution)/shard_map/forces/pallas_call | solution.py:630
  36.1 0.0 copy-start
  36.2 0.6 %copy-done = f32[3,1,1,16]{3,2,1,0:T(1,128)S(1)} copy-done((f32[3,1,1,16]{3,2,1,0:T(1,128)S(1)}, f32[3,1,1,16]{3,2,1,0:T(1,128)}, u32[]{:S(2)}) %copy-start) | copy-done | bytes 216
  36.8 0.0 copy-start.2
  36.8 0.6 %copy.22 = f32[3,1,1,16]{3,2,1,0:T(1,128)} copy(f32[3,1,1,16]{3,2,1,0:T(1,128)S(1)} %copy-done) | data formatting | bytes 384
  37.3 0.0 copy-done.2
  37.4 0.0 copy-start.1
  37.4 0.5 %copy.23 = f32[1,1,16]{2,1,0:T(1,128)} copy(f32[1,1,16]{2,1,0:T(1,128)S(1)} %copy-done.2) | data formatting | bytes 128
  37.9 0.1 copy-done.1
  38.0 0.5 %copy.24 = f32[1,1,16]{2,1,0:T(1,128)} copy(f32[1,1,16]{2,1,0:T(1,128)S(1)} %copy-done.1) | data formatting | bytes 128
Async XLA Ops:
  36.1 0.6 %copy-start = (f32[3,1,1,16]{3,2,1,0:T(1,128)S(1)}, f32[3,1,1,16]{3,2,1,0:T(1,128)}, u32[]{:S(2)}) copy-start(f32[3,1,1,16]{3,2,1,0:T(1,128)} %get-tuple-element.6) | copy-start | bytes 580
  36.8 0.6 %copy-start.2 = (f32[1,1,16]{2,1,0:T(1,128)S(1)}, f32[1,1,16]{2,1,0:T(1,128)}, u32[]{:S(2)}) copy-start(f32[1,1,16]{2,1,0:T(1,128)} %get-tuple-element.7) | copy-start | bytes 196
  37.4 0.6 %copy-start.1 = (f32[1,1,16]{2,1,0:T(1,128)S(1)}, f32[1,1,16]{2,1,0:T(1,128)}, u32[]{:S(2)}) copy-start(f32[1,1,16]{2,1,0:T(1,128)} %get-tuple-element.8) | copy-start | bytes 196

commit v2 on v1

--- a/solution.py
+++ b/solution.py
@@ -106,7 +106,7 @@
     mean_ref, force_ref, virial_ref,
     pos_all, list_all, nb_ref, scale_ref, shift_ref, mid_ref, midb_ref, outer_ref, outb_ref,
     f1_ref, f1b_ref, f2_ref, f2b_ref, f3_ref, f3b_ref, read_ref,
-    nscr, ptab, code_ref, f1p_ref, sel_ref, oh_ref, em_ref,
+    nscr, ptab, code_ref, to_ref, f1p_ref, sel_ref, oh_ref, em_ref,
     w2_ref, w3_ref, a2_ref, a3_ref,
     off_ref, inv_ref, there_ref, id_ref, cen_ref, e4h_ref, e4l_ref,
     t1_ref, s2_ref, s3_ref, h3_ref, ms_ref, bm_ref, d_ref, dd_ref, y_ref, dms_ref,
@@ -148,14 +148,33 @@
         copy = pltpu.make_async_copy(src, dst, local_sem.at[place])
         copy.start()
         fetched.append(copy)
+    for copy in fetched[:2]:
+        copy.wait()
+    pl.semaphore_wait(barrier, len(found) - 1 + models - 1)
+    shares = []
+    for slot, off in enumerate(found):
+        if off == 0:
+            continue
+        peer = lax.rem(me + count - off, count)
+        for ref, send, recv in ((pos_all, send_a, recv_a), (list_all, send_b, recv_b)):
+            copy = pltpu.make_async_remote_copy(
+                src_ref=ref.at[0],
+                dst_ref=ref.at[slot],
+                send_sem=send.at[slot],
+                recv_sem=recv.at[slot],
+                device_id={"space": peer},
+                device_id_type=MESH,
+            )
+            copy.start()
+            shares.append(copy)
+
     em_ref[...] = jnp.zeros_like(em_ref)
     th_ref[...] = jnp.zeros_like(th_ref)
     tl_ref[...] = jnp.zeros_like(tl_ref)
     nscr[...] = jnp.zeros_like(nscr)
     ptab[...] = jnp.zeros_like(ptab)
-    for copy in fetched[:9]:
+    for copy in fetched[2:9]:
         copy.wait()
-
     c1 = spread_of(g1, width, width, g1)
     r2 = spread_of(g2, 2 * width, width, g1)
     r3 = spread_of(g3, 4 * width, width, g1)
@@ -178,24 +197,6 @@
     a2_ref[...] = jnp.concatenate([w2t.astype(BF16), fold2], axis=1)
     a3_ref[...] = jnp.concatenate([w3t.astype(BF16), fold3], axis=1)
 
-    pl.semaphore_wait(barrier, len(found) - 1 + models - 1)
-    shares = []
-    for slot, off in enumerate(found):
-        if off == 0:
-            continue
-        peer = lax.rem(me + count - off, count)
-        for ref, send, recv in ((pos_all, send_a, recv_a), (list_all, send_b, recv_b)):
-            copy = pltpu.make_async_remote_copy(
-                src_ref=ref.at[0],
-                dst_ref=ref.at[slot],
-                send_sem=send.at[slot],
-                recv_sem=recv.at[slot],
-                device_id={"space": peer},
-                device_id_type=MESH,
-            )
-            copy.start()
-            shares.append(copy)
-
     nscr[:, 0:k_total] = nb_ref[...]
     lane = iota((rows, LANES), 1)
     own_row = iota((rows, LANES), 0)
@@ -225,32 +226,36 @@
 
     fetched[9].wait()
 
-    def order(step, carry):
-        source = iota((units * AXIS, 2 * LANES), 0)
-        col = iota((units * AXIS, 2 * LANES), 1)
-        unit = source >> 4
-        padded = unit
-        for a in range(1, 4):
-            padded = padded + jnp.where(unit >= a * width, g1 - width, 0)
-        target = padded + LANES * ((source & (AXIS - 1)) - 2 * step)
+    source = iota((units * AXIS, LANES), 0)
+    unit = source >> 4
+    padded = unit
+    for a in range(1, 4):
+        padded = padded + jnp.where(unit >= a * width, g1 - width, 0)
+    to_ref[...] = padded + LANES * (source & (AXIS - 1)) - iota((units * AXIS, LANES), 1)
+
+    def order(step):
+        target = to_ref[...]
+        pick = jnp.concatenate(
+            [hot(target == LANES * (2 * step)), hot(target == LANES * (2 * step + 1))], axis=1
+        )
         f1p_ref[:, pl.ds(pl.multiple_of(step * 2 * LANES, 2 * LANES), 2 * LANES)] = nn(
-            f1_ref[...], hot(target == col)
+            f1_ref[...], pick
         ).astype(BF16)
-        return carry
-
-    lax.fori_loop(0, AXIS // 2, order, 0)
+
+    for step in range(AXIS // 2):
+        order(step)
     sel_ref[...] = hot((iota(sel_ref.shape, 0) >> 7) == iota(sel_ref.shape, 1))
 
-    def own_hot(step, carry):
+    def own_hot(step):
         for inner in range(ROWS):
             r = step * ROWS + inner
             for tile in range(tiles):
-                at = pl.multiple_of((r * tiles + tile) * LANES, LANES)
+                at = slice((inner * tiles + tile) * LANES, (inner * tiles + tile + 1) * LANES)
                 which = member[tile][0:1] * rows + r
-                oh_ref[LANES : 2 * LANES, pl.ds(at, LANES)] = hot(iota((LANES, LANES), 0) == which)
-        return carry
-
-    lax.fori_loop(0, chunks, own_hot, 0)
+                oh_ref[step, LANES : 2 * LANES, at] = hot(iota((LANES, LANES), 0) == which)
+
+    for step in range(chunks):
+        own_hot(step)
     for copy in fetched[10:]:
         copy.wait()
 
@@ -353,47 +358,46 @@
     ]
     w2, w3 = w2_ref[...], w3_ref[...]
 
-    def forward(ch, carry):
-        lanes = pl.ds(pl.multiple_of(ch * span, span), span)
+    def forward(ch):
         inv = jnp.concatenate(
             [inv_ref[tile, pl.ds(ch * ROWS + inner, 1), :] for inner in range(ROWS) for tile in range(tiles)],
             axis=1,
         )
         t1 = jnp.tanh(scale_c * inv + shift_c)
-        t1_ref[:, lanes] = t1
+        t1_ref[ch] = t1
         h1 = t1.astype(BF16)
         h1f = h1.astype(F32)
         u2 = jnp.tanh(nn(w2, h1))
         h2 = (jnp.concatenate([h1f, h1f], axis=0) + u2).astype(BF16)
-        s2_ref[:, lanes] = (1.0 - u2 * u2).astype(BF16)
+        s2_ref[ch] = (1.0 - u2 * u2).astype(BF16)
         u3 = jnp.tanh(nn(w3, h2))
         h2f = h2.astype(F32)
         h3 = (jnp.concatenate([h2f, h2f], axis=0) + u3).astype(BF16)
-        s3_ref[:, lanes] = (1.0 - u3 * u3).astype(BF16)
-        h3_ref[:, lanes] = h3
+        s3_ref[ch] = (1.0 - u3 * u3).astype(BF16)
+        h3_ref[ch] = h3
         for inner in range(ROWS):
             r = ch * ROWS + inner
             for tile in range(tiles):
                 cut = slice(tile * LANES, (tile + 1) * LANES)
-                at = pl.ds(pl.multiple_of((r * tiles + tile) * LANES, LANES), LANES)
+                at = slice((inner * tiles + tile) * LANES, (inner * tiles + tile + 1) * LANES)
                 for part, ref in enumerate((e4h_ref, e4l_ref)):
                     value = ref[tile, pl.ds(pl.multiple_of(r * 8, 8), 8), :]
                     block = jnp.concatenate(
                         [jnp.where(pick, value, 0.0) for pick in picks[tile]], axis=0
                     ).astype(BF16)
                     size = 4 * group
-                    em_ref[part * pairs + inner * size : part * pairs + (inner + 1) * size, at] = block
+                    em_ref[ch, part * pairs + inner * size : part * pairs + (inner + 1) * size, at] = block
                     if part == 0:
-                        em_ref[2 * pairs + inner * size : 2 * pairs + (inner + 1) * size, at] = block
+                        em_ref[ch, 2 * pairs + inner * size : 2 * pairs + (inner + 1) * size, at] = block
                 ident = id_ref[tile, pl.ds(r, 1), :] & (LANES - 1)
-                oh_ref[0:LANES, at] = hot(iota((LANES, LANES), 0) == ident)
-        moment = nt(em_ref[0 : 2 * pairs, lanes], h3)
+                oh_ref[ch, 0:LANES, at] = hot(iota((LANES, LANES), 0) == ident)
+        moment = nt(em_ref[ch, 0 : 2 * pairs, :], h3)
         ms_ref[pl.ds(pl.multiple_of(ch * pairs, pairs), pairs), :] = (
             moment[0:pairs] + moment[pairs : 2 * pairs]
         )
-        return carry
-
-    lax.fori_loop(0, chunks, forward, 0)
+
+    for ch in range(chunks):
+        forward(ch)
 
     inverse_k = 1.0 / k_total
     mt = [ms_ref[pl.ds(c, owned, stride=4), :] * inverse_k for c in range(4)]
@@ -417,8 +421,8 @@
         pair = nn(both(value), weight)
         return rounded(pair[0:owned] + pair[owned : 2 * owned])
 
-    b2 = rounded(read + back(read * ((1.0 + u3) * (1.0 - u3)), f3_ref[...]))
-    b1 = rounded(b2 + back(b2 * ((1.0 + u2) * (1.0 - u2)), f2_ref[...]))
+    b2 = read + back(read * ((1.0 + u3) * (1.0 - u3)), f3_ref[...])
+    b1 = rounded(b2) + back(b2 * ((1.0 + u2) * (1.0 - u2)), f2_ref[...])
     dd_ref[...] = back(b1 * ((1.0 + u1) * (1.0 - u1)), f1p_ref[...])
 
     sums = [None] * 4
@@ -434,16 +438,15 @@
 
     a2, a3 = a2_ref[...], a3_ref[...]
 
-    def backward(ch, carry):
-        lanes = pl.ds(pl.multiple_of(ch * span, span), span)
+    def backward(ch):
         high, low = split(dms_ref[pl.ds(pl.multiple_of(ch * pairs, pairs), pairs), :], 2)
-        h3 = h3_ref[:, lanes]
-        d3 = tn(jnp.concatenate([high, high, low], axis=0), em_ref[:, lanes]).astype(BF16)
-        p3 = d3 * s3_ref[:, lanes]
+        h3 = h3_ref[ch]
+        d3 = tn(jnp.concatenate([high, high, low], axis=0), em_ref[ch]).astype(BF16)
+        p3 = d3 * s3_ref[ch]
         d2 = nn(a3, jnp.concatenate([p3, d3], axis=0)).astype(BF16)
-        p2 = d2 * s2_ref[:, lanes]
+        p2 = d2 * s2_ref[ch]
         d1 = nn(a2, jnp.concatenate([p2, d2], axis=0))
-        t1 = t1_ref[:, lanes]
+        t1 = t1_ref[ch]
         p1 = jnp.sum(d1 * (1.0 - t1 * t1) * scale_c, axis=0, keepdims=True)
         denv = nn(jnp.concatenate([high, low], axis=0), h3)
         denv = denv[0:pairs] + denv[pairs : 2 * pairs]
@@ -459,9 +462,9 @@
                     value = part if value is None else value + part
                 value = value + pltpu.roll(value, 4, 0)
                 de4_ref[tile, pl.ds(pl.multiple_of(r * 8, 8), 8), :] = value
-        return carry
-
-    lax.fori_loop(0, chunks, backward, 0)
+
+    for ch in range(chunks):
+        backward(ch)
 
     for tile in range(tiles):
         cut = slice(tile * LANES, (tile + 1) * LANES)
@@ -493,10 +496,11 @@
                     for m in range(masks_count):
                         first = (2 * m + part) * 16
                         lhs_ref[first : first + 16, at] = jnp.where(band == m, value, 0.0).astype(BF16)
-        lanes = pl.ds(pl.multiple_of(ch * span, span), span)
-        return sums + nt(lhs_ref[...], oh_ref[:, lanes])
-
-    sums = lax.fori_loop(0, chunks, scatter, jnp.zeros((32 * masks_count, 2 * LANES), F32))
+        return sums + nt(lhs_ref[...], oh_ref[ch])
+
+    sums = jnp.zeros((32 * masks_count, 2 * LANES), F32)
+    for ch in range(chunks):
+        sums = scatter(ch, sums)
     centre = jnp.zeros((16, LANES), F32)
     for m in range(masks_count):
         upper = sums[32 * m : 32 * m + 16]
@@ -593,12 +597,12 @@
     fit = f1.shape[1]
     group = LANES // math.gcd(k_total, LANES)
     rows = owned // group
-    all_pairs = owned * k_total
     row_lanes = group * k_total
     tiles = row_lanes // LANES
     pairs = ROWS * group * 4
     bands = (slots * owned + LANES - 1) // LANES
     span = ROWS * row_lanes
+    chunks = rows // ROWS
     args = (positions, lists, named, scale, shift, mid, midb, outer, outb, f1, f1b, f2, f2b, f3, f3b, read)
 
     def vm(shape, dtype=F32):
@@ -611,14 +615,15 @@
         vm((fit, units * AXIS), BF16), vm((1, fit)), vm((fit, fit), BF16), vm((1, fit)),
         vm((fit, fit), BF16), vm((1, fit)), vm((1, fit), BF16),
         vm((owned, LANES), I32), vm((bands, 8, LANES)), vm((64, LANES), I32),
+        vm((units * AXIS, LANES), I32),
         vm((fit, AXIS * LANES), BF16), vm((AXIS * LANES, LANES), BF16),
-        vm((2 * LANES, all_pairs), BF16), vm((3 * pairs, all_pairs), BF16),
+        vm((chunks, 2 * LANES, span), BF16), vm((chunks, 3 * pairs, span), BF16),
         vm((64, 32), BF16), vm((128, 64), BF16), vm((32, 128), BF16), vm((64, 256), BF16),
         vm((3, rows, row_lanes)), vm((tiles, rows, LANES)), vm((rows, row_lanes)),
         vm((tiles, rows, LANES), I32), vm((3, rows, row_lanes)),
         vm((tiles, 8 * rows, LANES)), vm((tiles, 8 * rows, LANES)),
-        vm((32, all_pairs)), vm((64, all_pairs), BF16), vm((128, all_pairs), BF16),
-        vm((128, all_pairs), BF16), vm((4 * owned, LANES)), vm((4 * AXIS, owned, LANES)),
+        vm((chunks, 32, span)), vm((chunks, 64, span), BF16), vm((chunks, 128, span), BF16),
+        vm((chunks, 128, span), BF16), vm((4 * owned, LANES)), vm((4 * AXIS, owned, LANES)),
         vm((owned, AXIS * LANES), BF16), vm((owned, AXIS * LANES)),
         vm((4 * owned, AXIS * LANES), BF16), vm((4 * owned, LANES)),
         vm((tiles, 8 * rows, LANES)), vm((tiles, rows, LANES)),

time: 38.7 us -> 29.6 us (0.76)
  Pallas kernels: 35.5 us -> 26.4 us
    pallas_call x1, Pallas kernels: 35.5 us -> 26.4 us  [local(): pl.pallas_call(functools.partial(kernel, count, models, strides, found, (...]
where the time goes in v2:
time: 29.6 us; the launch traced here: 29.4 us
  Pallas kernels  26.4 us (89%)
  local copies, waits for them, and re-layouts  2.34 us (8%)
  between operations  0.66 us (2%)
    pallas_call x1, Pallas kernels, local(): pl.pallas_call(functools.partial(kernel, count, models, strides, found, (...  26.4 us
    unnamed x9, local copies, waits for them, and re-layouts  2.34 us

profile of v2, /device:TPU:0, one launch (start us, length us, event | category | flops | bytes accessed | tf_op | source)
XLA Modules:
  0.0 29.4 jit_solution(14294062334346080400)
XLA Ops:
  0.6 26.4 %forces.1 = (f32[3,1,1,16]{3,2,1,0:T(1,128)}, f32[1,1,16]{2,1,0:T(1,128)}, f32[1,1,16]{2,1,0:T(1,128)}) custom-call(f32[3,64]{1,0:T(4,128)} %pos_in.1, s32[6,1,128]{2,1,0:T(1,128)} %bitcast.7, s32[64,96]{1,0:T(8,128)} %bitcast.4, f32[1,25]{1,0:T(1,128)} %scale_in.1, f32[1,25]{1,0:T(1,128)} %shift_in.1, bf16[1,25,50]{2,1,0:T(8,128)(2,1)} %bitcast.6, ...), custom_call_target="tpu_custom_call" | custom-call | tf_op jit(solution)/shard_map/forces/pallas_call | solution.py:635
  27.0 0.0 copy-start
  27.1 0.6 %copy-done = f32[3,1,1,16]{3,2,1,0:T(1,128)S(1)} copy-done((f32[3,1,1,16]{3,2,1,0:T(1,128)S(1)}, f32[3,1,1,16]{3,2,1,0:T(1,128)}, u32[]{:S(2)}) %copy-start) | copy-done | bytes 216
  27.7 0.0 copy-start.2
  27.7 0.6 %copy.22 = f32[3,1,1,16]{3,2,1,0:T(1,128)} copy(f32[3,1,1,16]{3,2,1,0:T(1,128)S(1)} %copy-done) | data formatting | bytes 384
  28.2 0.0 copy-done.2
  28.3 0.0 copy-start.1
  28.3 0.5 %copy.23 = f32[1,1,16]{2,1,0:T(1,128)} copy(f32[1,1,16]{2,1,0:T(1,128)S(1)} %copy-done.2) | data formatting | bytes 128
  28.8 0.1 copy-done.1
  28.9 0.5 %copy.24 = f32[1,1,16]{2,1,0:T(1,128)} copy(f32[1,1,16]{2,1,0:T(1,128)S(1)} %copy-done.1) | data formatting | bytes 128
Async XLA Ops:
  27.0 0.6 %copy-start = (f32[3,1,1,16]{3,2,1,0:T(1,128)S(1)}, f32[3,1,1,16]{3,2,1,0:T(1,128)}, u32[]{:S(2)}) copy-start(f32[3,1,1,16]{3,2,1,0:T(1,128)} %get-tuple-element.6) | copy-start | bytes 580
  27.7 0.6 %copy-start.2 = (f32[1,1,16]{2,1,0:T(1,128)S(1)}, f32[1,1,16]{2,1,0:T(1,128)}, u32[]{:S(2)}) copy-start(f32[1,1,16]{2,1,0:T(1,128)} %get-tuple-element.7) | copy-start | bytes 196
  28.3 0.6 %copy-start.1 = (f32[1,1,16]{2,1,0:T(1,128)S(1)}, f32[1,1,16]{2,1,0:T(1,128)}, u32[]{:S(2)}) copy-start(f32[1,1,16]{2,1,0:T(1,128)} %get-tuple-element.8) | copy-start | bytes 196

commit v3 on v2

--- a/solution.py
+++ b/solution.py
@@ -103,15 +103,15 @@
     pos_in, list_in, nb_in,
     scale_in, shift_in, mid_in, midb_in, outer_in, outb_in,
     f1_in, f1b_in, f2_in, f2b_in, f3_in, f3b_in, read_in,
-    mean_ref, force_ref, virial_ref,
+    out_ref,
     pos_all, list_all, nb_ref, scale_ref, shift_ref, mid_ref, midb_ref, outer_ref, outb_ref,
     f1_ref, f1b_ref, f2_ref, f2b_ref, f3_ref, f3b_ref, read_ref,
     nscr, ptab, code_ref, to_ref, f1p_ref, sel_ref, oh_ref, em_ref,
     w2_ref, w3_ref, a2_ref, a3_ref,
     off_ref, inv_ref, there_ref, id_ref, cen_ref, e4h_ref, e4l_ref,
     t1_ref, s2_ref, s3_ref, h3_ref, ms_ref, bm_ref, d_ref, dd_ref, y_ref, dms_ref,
-    de4_ref, di_ref, th_ref, tl_ref, lhs_ref, part_ref, held, total, others,
-    local_sem, send_a, recv_a, send_b, recv_b, send_c, recv_c, send_d, recv_d,
+    de4_ref, di_ref, th_ref, tl_ref, lhs_ref, mess_ref, held,
+    local_sem, send_a, recv_a, send_b, recv_b, send_c, recv_c,
 ):
     owned, k_total, width, fit = sizes
     slots = len(found)
@@ -501,81 +501,85 @@
     sums = jnp.zeros((32 * masks_count, 2 * LANES), F32)
     for ch in range(chunks):
         sums = scatter(ch, sums)
-    centre = jnp.zeros((16, LANES), F32)
+    quarter = owned // models
+    blocks = LANES // quarter
+    lane8 = iota((8, LANES), 1)
+    sub = iota((8, LANES), 0)
+    spot = lane8 % quarter
+    block = lane8 // quarter
+
+    def across(value):
+        value = jnp.take_along_axis(
+            value, ((block - sub) & (blocks - 1)) * quarter + spot, axis=1, mode="promise_in_bounds"
+        )
+        value = jnp.take_along_axis(value, (block - sub) & (blocks - 1), axis=0, mode="promise_in_bounds")
+        return jnp.take_along_axis(
+            value, ((block + sub) & (blocks - 1)) * quarter + spot, axis=1, mode="promise_in_bounds"
+        )
+
+    centre = jnp.zeros((8, LANES), F32)
+    wholes = []
     for m in range(masks_count):
-        upper = sums[32 * m : 32 * m + 16]
-        lower = sums[32 * m + 16 : 32 * m + 32]
-        whole = upper + lower
-        part_ref[m] = whole[:, 0:LANES]
-        centre = centre + whole[:, LANES : 2 * LANES]
-    centre = jnp.where(iota((16, LANES), 0) < 3, centre, 0.0)
-    mine = part_ref[0] - centre
+        whole = sums[32 * m : 32 * m + 16] + sums[32 * m + 16 : 32 * m + 32]
+        centre = centre + whole[0:8, LANES : 2 * LANES]
+        wholes.append([whole[0:8, 0:LANES], whole[8:16, 0:LANES]])
+    wholes[0][0] = wholes[0][0] - jnp.where(sub < 3, centre, 0.0)
+    for m in range(masks_count):
+        for half in range(2):
+            turned_block = across(wholes[m][half])
+            for at in range(blocks):
+                mess_ref[m * blocks + at, half : half + 1, :] = turned_block[at : at + 1, :]
 
     sent = []
     for slot, off in enumerate(found):
-        if off == 0:
-            continue
-        copy = pltpu.make_async_remote_copy(
-            src_ref=part_ref.at[(slot * owned) // LANES],
-            dst_ref=held.at[slot],
-            send_sem=send_c.at[slot],
-            recv_sem=recv_c.at[slot],
-            device_id={"space": lax.rem(me + off, count)},
-            device_id_type=MESH,
-        )
-        copy.start()
-        sent.append(copy)
+        for step in range(models):
+            if off == 0 and step == 0:
+                continue
+            to = lax.rem(model + step, models)
+            index = step * slots + slot
+            copy = pltpu.make_async_remote_copy(
+                src_ref=mess_ref.at[slot * models + to],
+                dst_ref=held.at[index],
+                send_sem=send_c.at[index],
+                recv_sem=recv_c.at[index],
+                device_id={"mp": to, "space": lax.rem(me + off, count)},
+                device_id_type=MESH,
+            )
+            copy.start()
+            sent.append(copy)
     for copy in sent:
         copy.wait_recv()
-    per = LANES // owned
-    lots = [None] * per
-    for slot in range(slots):
-        value = mine if slot == 0 else held[slot]
-        lots[slot % per] = value if lots[slot % per] is None else lots[slot % per] + value
-    own = lots[0]
-    for at in range(1, per):
-        own = own + pltpu.roll(lots[at], LANES - at * owned, 1)
-    total[...] = own
-    last = []
-    for step in range(1, models):
-        copy = pltpu.make_async_remote_copy(
-            src_ref=total,
-            dst_ref=others.at[step],
-            send_sem=send_d.at[step],
-            recv_sem=recv_d.at[step],
-            device_id={"mp": lax.rem(model + step, models)},
-            device_id_type=MESH,
-        )
-        copy.start()
-        last.append(copy)
-    for copy in shares + sent:
-        copy.wait_send()
-    for copy in last:
-        copy.wait_recv()
-    stacked = [own] + [others[step] for step in range(1, models)]
+    stacked = []
+    for step in range(models):
+        value = mess_ref[model] if step == 0 else held[step * slots]
+        for slot in range(1, slots):
+            value = value + held[step * slots + slot]
+        stacked.append(value)
     mean = sum(stacked[1:], stacked[0]) * (1.0 / models)
     square = jnp.zeros_like(mean)
     for one in stacked:
         square = square + (one - mean) * (one - mean)
     square = square * (1.0 / models)
-    row = iota(square.shape, 0)
-    force = jnp.sum(jnp.where(row < 3, square, 0.0), axis=0, keepdims=True)
-    virial = jnp.sum(jnp.where((row >= 3) & (row < 12), square, 0.0), axis=0, keepdims=True)
-    quarter = owned // models
-
-    def pick_mine(value):
-        result = value[:, 0:quarter]
-        for part in range(1, models):
-            result = jnp.where(model == part, value[:, part * quarter : (part + 1) * quarter], result)
-        return result
-
-    means = pick_mine(mean[0:3])
+    part_of = iota((1, LANES), 1) // quarter
+    force = jnp.where(part_of < 3, square[0:1], 0.0)
+    virial = jnp.where(part_of >= 3, square[0:1], 0.0) + jnp.where(part_of < 12 - blocks, square[1:2], 0.0)
+    two = jnp.concatenate([force, virial], axis=0)
+    reach = LANES // 2
+    while reach >= quarter:
+        two = two + pltpu.roll(two, reach, 1)
+        reach //= 2
+    out_ref[0:1, :] = mean[0:1]
+    out_ref[1:3, :] = two
+    for copy in shares + sent:
+        copy.wait_send()
+
+
+def settle(out_in, mean_ref, force_ref, virial_ref):
+    quarter = mean_ref.shape[-1]
     for c in range(3):
-        mean_ref[c, 0] = means[c : c + 1]
-    force_ref[0] = pick_mine(force)
-    virial_ref[0] = pick_mine(virial)
-    for copy in last:
-        copy.wait_send()
+        mean_ref[c, 0] = out_in[0:1, c * quarter : (c + 1) * quarter]
+    force_ref[0] = out_in[1:2, 0:quarter]
+    virial_ref[0] = out_in[2:3, 0:quarter]
 
 
 def local(positions, send_lists, neighbours, *weights):
@@ -628,27 +632,35 @@
         vm((4 * owned, AXIS * LANES), BF16), vm((4 * owned, LANES)),
         vm((tiles, 8 * rows, LANES)), vm((tiles, rows, LANES)),
         vm((tiles, 16 * rows, LANES)), vm((tiles, 16 * rows, LANES)), vm((32 * bands, span), BF16),
-        vm((bands, 16, LANES)), vm((slots, 16, LANES)), vm((16, LANES)), vm((models, 16, LANES)),
+        vm((bands * (LANES // quarter), 2, LANES)), vm((slots * models, 2, LANES)),
         pltpu.SemaphoreType.DMA((len(args),)),
     ]
-    scratch += [pltpu.SemaphoreType.DMA((slots,))] * 6 + [pltpu.SemaphoreType.DMA((models,))] * 2
-    return pl.pallas_call(
+    scratch += [pltpu.SemaphoreType.DMA((slots,))] * 4
+    scratch += [pltpu.SemaphoreType.DMA((slots * models,))] * 2
+    packed = pl.pallas_call(
         functools.partial(
             kernel, count, models, strides, found, (owned, k_total, width, fit)
         ),
-        out_shape=(
-            jax.ShapeDtypeStruct((3, 1, 1, quarter), F32),
-            jax.ShapeDtypeStruct((1, 1, quarter), F32),
-            jax.ShapeDtypeStruct((1, 1, quarter), F32),
-        ),
+        out_shape=jax.ShapeDtypeStruct((3, LANES), F32),
         in_specs=[ANY] * len(args),
-        out_specs=(VM, VM, VM),
+        out_specs=VM,
         scratch_shapes=scratch,
         compiler_params=pltpu.CompilerParams(
             collective_id=0, has_side_effects=True, vmem_limit_bytes=60000000
         ),
         name="forces",
     )(*args)
+    return pl.pallas_call(
+        settle,
+        out_shape=(
+            jax.ShapeDtypeStruct((3, 1, 1, quarter), F32),
+            jax.ShapeDtypeStruct((1, 1, quarter), F32),
+            jax.ShapeDtypeStruct((1, 1, quarter), F32),
+        ),
+        in_specs=[VM],
+        out_specs=(VM, VM, VM),
+        name="settle",
+    )(packed)
 
 
 def solution(mesh):

time: 29.6 us -> 26.8 us (0.905)
  local copies, waits for them, and re-layouts: 2.34 us -> 0 us
  Pallas kernels: 26.4 us -> 26 us
    unnamed x9 -> x0, local copies, waits for them, and re-layouts: 2.34 us -> none
    pallas_call x1, Pallas kernels: 26.4 us -> 24.7 us  [local(): pl.pallas_call(functools.partial(kernel, count, models, strides, found, (...]
    pallas_call x0 -> x1, Pallas kernels: none -> 1.32 us  [local(): pl.pallas_call(settle, out_shape=(jax.ShapeDtypeStruct((3, 1, 1, quarter)...]
where the time goes in v3:
time: 26.8 us; the launch traced here: 26.7 us
  Pallas kernels  26 us (97%)
  between operations  0.65 us (2%)
    pallas_call x1, Pallas kernels, local(): pl.pallas_call(functools.partial(kernel, count, models, strides, found, (...  24.7 us
    pallas_call x1, Pallas kernels, local(): pl.pallas_call(settle, out_shape=(jax.ShapeDtypeStruct((3, 1, 1, quarter)...  1.32 us

profile of v3, /device:TPU:0, one launch (start us, length us, event | category | flops | bytes accessed | tf_op | source)
XLA Modules:
  0.0 26.7 jit_solution(13488373782589936121)
XLA Ops:
  0.6 24.7 %forces.1.out_in = f32[3,128]{1,0:T(4,128)} custom-call(f32[3,64]{1,0:T(4,128)} %pos_in.1, s32[6,1,128]{2,1,0:T(1,128)} %bitcast.7, s32[64,96]{1,0:T(8,128)} %bitcast.4, f32[1,25]{1,0:T(1,128)} %scale_in.1, f32[1,25]{1,0:T(1,128)} %shift_in.1, bf16[1,25,50]{2,1,0:T(8,128)(2,1)} %bitcast.6, f32[1,50]{1,0:T(1,128)} %midb_in.1, bf16[1,50,100]{2,1,0:T(8,128)(2,1)} %bitcast.5, ...), custom_call_target="tpu_custom_call" | custom-call | tf_op jit(solution)/shard_map/forces/pallas_call | solution.py:640
  25.4 1.3 %settle.1 = (f32[3,1,1,16]{3,2,1,0:T(1,128)}, f32[1,1,16]{2,1,0:T(1,128)}, f32[1,1,16]{2,1,0:T(1,128)}) custom-call(f32[3,128]{1,0:T(4,128)} %forces.1.out_in), custom_call_target="tpu_custom_call" | custom-call | tf_op jit(solution)/shard_map/settle/pallas_call | solution.py:653

commit v4 on v3

--- a/solution.py
+++ b/solution.py
@@ -109,7 +109,7 @@
     nscr, ptab, code_ref, to_ref, f1p_ref, sel_ref, oh_ref, em_ref,
     w2_ref, w3_ref, a2_ref, a3_ref,
     off_ref, inv_ref, there_ref, id_ref, cen_ref, e4h_ref, e4l_ref,
-    t1_ref, s2_ref, s3_ref, h3_ref, ms_ref, bm_ref, d_ref, dd_ref, y_ref, dms_ref,
+    t1_ref, s2_ref, s3_ref, h3_ref, h1_ref, h2_ref, b3_ref, b2_ref, ms_ref, bm_ref, d_ref, dd_ref, y_ref, dms_ref,
     de4_ref, di_ref, th_ref, tl_ref, lhs_ref, mess_ref, held,
     local_sem, send_a, recv_a, send_b, recv_b, send_c, recv_c,
 ):
@@ -192,8 +192,8 @@
     w3t = nn(nn(hot(r2), outer_t).astype(BF16), wide3)
     w2_ref[...] = with_bias(w2, bias2_c, width)
     w3_ref[...] = with_bias(w3, bias3_c, width)
-    fold2 = hot(iota((g1, g2), 1) % g1 == iota((g1, g2), 0))
-    fold3 = hot(iota((g2, g3), 1) % g2 == iota((g2, g3), 0))
+    fold2 = hot(iota((g1, g1), 1) == iota((g1, g1), 0))
+    fold3 = hot(iota((g2, g2), 1) == iota((g2, g2), 0))
     a2_ref[...] = jnp.concatenate([w2t.astype(BF16), fold2], axis=1)
     a3_ref[...] = jnp.concatenate([w3t.astype(BF16), fold3], axis=1)
 
@@ -246,16 +246,6 @@
         order(step)
     sel_ref[...] = hot((iota(sel_ref.shape, 0) >> 7) == iota(sel_ref.shape, 1))
 
-    def own_hot(step):
-        for inner in range(ROWS):
-            r = step * ROWS + inner
-            for tile in range(tiles):
-                at = slice((inner * tiles + tile) * LANES, (inner * tiles + tile + 1) * LANES)
-                which = member[tile][0:1] * rows + r
-                oh_ref[step, LANES : 2 * LANES, at] = hot(iota((LANES, LANES), 0) == which)
-
-    for step in range(chunks):
-        own_hot(step)
     for copy in fetched[10:]:
         copy.wait()
 
@@ -358,23 +348,34 @@
     ]
     w2, w3 = w2_ref[...], w3_ref[...]
 
-    def forward(ch):
+    def first_layer(ch):
         inv = jnp.concatenate(
-            [inv_ref[tile, pl.ds(ch * ROWS + inner, 1), :] for inner in range(ROWS) for tile in range(tiles)],
+            [
+                inv_ref[tile, ch * ROWS + inner : ch * ROWS + inner + 1, :]
+                for inner in range(ROWS)
+                for tile in range(tiles)
+            ],
             axis=1,
         )
         t1 = jnp.tanh(scale_c * inv + shift_c)
         t1_ref[ch] = t1
-        h1 = t1.astype(BF16)
+        h1_ref[ch] = t1.astype(BF16)
+
+    def second_layer(ch):
+        h1 = h1_ref[ch]
         h1f = h1.astype(F32)
         u2 = jnp.tanh(nn(w2, h1))
-        h2 = (jnp.concatenate([h1f, h1f], axis=0) + u2).astype(BF16)
+        h2_ref[ch] = (jnp.concatenate([h1f, h1f], axis=0) + u2).astype(BF16)
         s2_ref[ch] = (1.0 - u2 * u2).astype(BF16)
+
+    def third_layer(ch):
+        h2 = h2_ref[ch]
         u3 = jnp.tanh(nn(w3, h2))
         h2f = h2.astype(F32)
-        h3 = (jnp.concatenate([h2f, h2f], axis=0) + u3).astype(BF16)
+        h3_ref[ch] = (jnp.concatenate([h2f, h2f], axis=0) + u3).astype(BF16)
         s3_ref[ch] = (1.0 - u3 * u3).astype(BF16)
-        h3_ref[ch] = h3
+
+    def envelopes(ch):
         for inner in range(ROWS):
             r = ch * ROWS + inner
             for tile in range(tiles):
@@ -389,15 +390,14 @@
                     em_ref[ch, part * pairs + inner * size : part * pairs + (inner + 1) * size, at] = block
                     if part == 0:
                         em_ref[ch, 2 * pairs + inner * size : 2 * pairs + (inner + 1) * size, at] = block
-                ident = id_ref[tile, pl.ds(r, 1), :] & (LANES - 1)
-                oh_ref[ch, 0:LANES, at] = hot(iota((LANES, LANES), 0) == ident)
-        moment = nt(em_ref[ch, 0 : 2 * pairs, :], h3)
-        ms_ref[pl.ds(pl.multiple_of(ch * pairs, pairs), pairs), :] = (
-            moment[0:pairs] + moment[pairs : 2 * pairs]
-        )
-
-    for ch in range(chunks):
-        forward(ch)
+
+    def moments(ch):
+        moment = nt(em_ref[ch, 0 : 2 * pairs, :], h3_ref[ch])
+        ms_ref[ch * pairs : (ch + 1) * pairs, :] = moment[0:pairs] + moment[pairs : 2 * pairs]
+
+    for stage in (first_layer, second_layer, envelopes, third_layer, moments):
+        for ch in range(chunks):
+            stage(ch)
 
     inverse_k = 1.0 / k_total
     mt = [ms_ref[pl.ds(c, owned, stride=4), :] * inverse_k for c in range(4)]
@@ -410,11 +410,27 @@
             total_p = part if total_p is None else total_p + part
         d_ref[:, p * LANES : (p + 1) * LANES] = total_p.astype(BF16)
 
+    def one_hots(step):
+        for inner in range(ROWS):
+            r = step * ROWS + inner
+            for tile in range(tiles):
+                at = slice((inner * tiles + tile) * LANES, (inner * tiles + tile + 1) * LANES)
+                which = member[tile][0:1] * rows + r
+                ident = id_ref[tile, pl.ds(r, 1), :] & (LANES - 1)
+                oh_ref[step, 0:LANES, at] = hot(iota((LANES, LANES), 0) == ident)
+                oh_ref[step, LANES : 2 * LANES, at] = hot(iota((LANES, LANES), 0) == which)
+
     u1 = jnp.tanh(nt(d_ref[...], f1p_ref[...]) + f1b_ref[...])
+    for step in range(chunks * 0 // 8, chunks * 2 // 8):
+        one_hots(step)
     q1 = u1.astype(BF16)
     u2 = jnp.tanh(nt(q1, f2_ref[...]) + f2b_ref[...])
+    for step in range(chunks * 2 // 8, chunks * 4 // 8):
+        one_hots(step)
     q2 = (q1.astype(F32) + u2).astype(BF16)
     u3 = jnp.tanh(nt(q2, f3_ref[...]) + f3b_ref[...])
+    for step in range(chunks * 4 // 8, chunks * 5 // 8):
+        one_hots(step)
     read = read_ref[...].astype(F32)
 
     def back(value, weight):
@@ -422,8 +438,14 @@
         return rounded(pair[0:owned] + pair[owned : 2 * owned])
 
     b2 = read + back(read * ((1.0 + u3) * (1.0 - u3)), f3_ref[...])
+    for step in range(chunks * 5 // 8, chunks * 6 // 8):
+        one_hots(step)
     b1 = rounded(b2) + back(b2 * ((1.0 + u2) * (1.0 - u2)), f2_ref[...])
+    for step in range(chunks * 6 // 8, chunks * 7 // 8):
+        one_hots(step)
     dd_ref[...] = back(b1 * ((1.0 + u1) * (1.0 - u1)), f1p_ref[...])
+    for step in range(chunks * 7 // 8, chunks * 8 // 8):
+        one_hots(step)
 
     sums = [None] * 4
     for p in range(AXIS):
@@ -438,33 +460,44 @@
 
     a2, a3 = a2_ref[...], a3_ref[...]
 
-    def backward(ch):
-        high, low = split(dms_ref[pl.ds(pl.multiple_of(ch * pairs, pairs), pairs), :], 2)
-        h3 = h3_ref[ch]
+    def back_outer(ch):
+        high, low = split(dms_ref[ch * pairs : (ch + 1) * pairs, :], 2)
         d3 = tn(jnp.concatenate([high, high, low], axis=0), em_ref[ch]).astype(BF16)
-        p3 = d3 * s3_ref[ch]
-        d2 = nn(a3, jnp.concatenate([p3, d3], axis=0)).astype(BF16)
-        p2 = d2 * s2_ref[ch]
-        d1 = nn(a2, jnp.concatenate([p2, d2], axis=0))
-        t1 = t1_ref[ch]
-        p1 = jnp.sum(d1 * (1.0 - t1 * t1) * scale_c, axis=0, keepdims=True)
-        denv = nn(jnp.concatenate([high, low], axis=0), h3)
+        b3_ref[ch, 0:g3] = d3 * s3_ref[ch]
+        b3_ref[ch, g3 : g3 + g2] = d3[0:g2] + d3[g2:g3]
+
+    def back_env(ch):
+        denv = nn(both(dms_ref[ch * pairs : (ch + 1) * pairs, :]), h3_ref[ch])
         denv = denv[0:pairs] + denv[pairs : 2 * pairs]
         for inner in range(ROWS):
             r = ch * ROWS + inner
             for tile in range(tiles):
                 at = (inner * tiles + tile) * LANES
-                di_ref[tile, pl.ds(r, 1), :] = p1[:, at : at + LANES]
                 value = None
                 for v, pick in enumerate(picks[tile]):
                     first = inner * 4 * group + 8 * v
                     part = jnp.where(pick, denv[first : first + 8, at : at + LANES], 0.0)
                     value = part if value is None else value + part
                 value = value + pltpu.roll(value, 4, 0)
-                de4_ref[tile, pl.ds(pl.multiple_of(r * 8, 8), 8), :] = value
-
-    for ch in range(chunks):
-        backward(ch)
+                de4_ref[tile, r * 8 : (r + 1) * 8, :] = value
+
+    def back_middle(ch):
+        d2 = nn(a3, b3_ref[ch]).astype(BF16)
+        b2_ref[ch, 0:g2] = d2 * s2_ref[ch]
+        b2_ref[ch, g2 : g2 + g1] = d2[0:g1] + d2[g1:g2]
+
+    def back_inner(ch):
+        d1 = nn(a2, b2_ref[ch])
+        t1 = t1_ref[ch]
+        p1 = jnp.sum(d1 * (1.0 - t1 * t1) * scale_c, axis=0, keepdims=True)
+        for inner in range(ROWS):
+            for tile in range(tiles):
+                at = (inner * tiles + tile) * LANES
+                di_ref[tile, ch * ROWS + inner : ch * ROWS + inner + 1, :] = p1[:, at : at + LANES]
+
+    for stage in (back_outer, back_middle, back_env, back_inner):
+        for ch in range(chunks):
+            stage(ch)
 
     for tile in range(tiles):
         cut = slice(tile * LANES, (tile + 1) * LANES)
@@ -484,7 +517,7 @@
             th_ref[tile, pl.ds(at, rows, stride=16), :] = high
             tl_ref[tile, pl.ds(at, rows, stride=16), :] = term - high
 
-    def scatter(ch, sums):
+    def banded(ch):
         for inner in range(ROWS):
             r = ch * ROWS + inner
             for tile in range(tiles):
@@ -495,12 +528,13 @@
                     value = ref[tile, pl.ds(pl.multiple_of(r * 16, 16), 16), :]
                     for m in range(masks_count):
                         first = (2 * m + part) * 16
-                        lhs_ref[first : first + 16, at] = jnp.where(band == m, value, 0.0).astype(BF16)
-        return sums + nt(lhs_ref[...], oh_ref[ch])
+                        lhs_ref[ch, first : first + 16, at] = jnp.where(band == m, value, 0.0).astype(BF16)
 
     sums = jnp.zeros((32 * masks_count, 2 * LANES), F32)
     for ch in range(chunks):
-        sums = scatter(ch, sums)
+        banded(ch)
+    for ch in range(chunks):
+        sums = sums + nt(lhs_ref[ch], oh_ref[ch])
     quarter = owned // models
     blocks = LANES // quarter
     lane8 = iota((8, LANES), 1)
@@ -622,16 +656,17 @@
         vm((units * AXIS, LANES), I32),
         vm((fit, AXIS * LANES), BF16), vm((AXIS * LANES, LANES), BF16),
         vm((chunks, 2 * LANES, span), BF16), vm((chunks, 3 * pairs, span), BF16),
-        vm((64, 32), BF16), vm((128, 64), BF16), vm((32, 128), BF16), vm((64, 256), BF16),
+        vm((64, 32), BF16), vm((128, 64), BF16), vm((32, 96), BF16), vm((64, 192), BF16),
         vm((3, rows, row_lanes)), vm((tiles, rows, LANES)), vm((rows, row_lanes)),
         vm((tiles, rows, LANES), I32), vm((3, rows, row_lanes)),
         vm((tiles, 8 * rows, LANES)), vm((tiles, 8 * rows, LANES)),
         vm((chunks, 32, span)), vm((chunks, 64, span), BF16), vm((chunks, 128, span), BF16),
-        vm((chunks, 128, span), BF16), vm((4 * owned, LANES)), vm((4 * AXIS, owned, LANES)),
+        vm((chunks, 128, span), BF16), vm((chunks, 32, span), BF16), vm((chunks, 64, span), BF16),
+        vm((chunks, 192, span), BF16), vm((chunks, 96, span), BF16), vm((4 * owned, LANES)), vm((4 * AXIS, owned, LANES)),
         vm((owned, AXIS * LANES), BF16), vm((owned, AXIS * LANES)),
         vm((4 * owned, AXIS * LANES), BF16), vm((4 * owned, LANES)),
         vm((tiles, 8 * rows, LANES)), vm((tiles, rows, LANES)),
-        vm((tiles, 16 * rows, LANES)), vm((tiles, 16 * rows, LANES)), vm((32 * bands, span), BF16),
+        vm((tiles, 16 * rows, LANES)), vm((tiles, 16 * rows, LANES)), vm((chunks, 32 * bands, span), BF16),
         vm((bands * (LANES // quarter), 2, LANES)), vm((slots * models, 2, LANES)),
         pltpu.SemaphoreType.DMA((len(args),)),
     ]

time: 26.8 us -> 24.4 us (0.910)
  Pallas kernels: 26 us -> 23.6 us
    pallas_call x1, Pallas kernels: 24.7 us -> 22.2 us  [local(): pl.pallas_call(functools.partial(kernel, count, models, strides, found, (...]
where the time goes in v4:
time: 24.4 us; the launch traced here: 24.2 us
  Pallas kernels  23.6 us (97%)
  between operations  0.65 us (3%)
    pallas_call x1, Pallas kernels, local(): pl.pallas_call(functools.partial(kernel, count, models, strides, found, (...  22.2 us
    pallas_call x1, Pallas kernels, local(): pl.pallas_call(settle, out_shape=(jax.ShapeDtypeStruct((3, 1, 1, quarter)...  1.32 us

profile of v4, /device:TPU:0, one launch (start us, length us, event | category | flops | bytes accessed | tf_op | source)
XLA Modules:
  0.0 24.2 jit_solution(15094192191460265773)
XLA Ops:
  0.6 22.2 %forces.1.out_in = f32[3,128]{1,0:T(4,128)} custom-call(f32[3,64]{1,0:T(4,128)} %pos_in.1, s32[6,1,128]{2,1,0:T(1,128)} %bitcast.7, s32[64,96]{1,0:T(8,128)} %bitcast.4, f32[1,25]{1,0:T(1,128)} %scale_in.1, f32[1,25]{1,0:T(1,128)} %shift_in.1, bf16[1,25,50]{2,1,0:T(8,128)(2,1)} %bitcast.6, f32[1,50]{1,0:T(1,128)} %midb_in.1, bf16[1,50,100]{2,1,0:T(8,128)(2,1)} %bitcast.5, ...), custom_call_target="tpu_custom_call" | custom-call | tf_op jit(solution)/shard_map/forces/pallas_call | solution.py:675
  22.9 1.3 %settle.1 = (f32[3,1,1,16]{3,2,1,0:T(1,128)}, f32[1,1,16]{2,1,0:T(1,128)}, f32[1,1,16]{2,1,0:T(1,128)}) custom-call(f32[3,128]{1,0:T(4,128)} %forces.1.out_in), custom_call_target="tpu_custom_call" | custom-call | tf_op jit(solution)/shard_map/settle/pallas_call | solution.py:688
